TPU v7x, 512 devices: a whole 4x4x16 slice. The times are simulated.
512 devices in a mesh: grp: 64 (over z, x), head: 8 (over y, core).
Axes of the slice: x: 4, y: 4, z: 16, core: 2. Of those that a mesh axis runs over, the one named last changes fastest.
Arguments:
- residual: bfloat16 [1024, 2880], P('grp'), may hold values from -4 to 4
- queries: bfloat16 [1024, 8, 256], P('grp', 'head'), may hold values from -200 to 200
- kv_cache: bfloat16 [1024, 8, 128, 128], P('grp', 'head'), may hold values from -5 to 5
- new_kv: bfloat16 [1024, 8, 128], P('grp', 'head'), may hold values from -5 to 5
- positions: int32 [1024], P('grp'), may hold values from 0 to 383
- sink_logits: float32 [8, 4], P('head'), may hold values from 0 to 5
- out_proj: bfloat16 [8, 256, 2880], P('head'), may hold values from -0.375 to 0.375
- norm_gain: float32 [2880], replicated, may hold values from 0.5 to 1.5
- route_ids: int32 [1024, 4], P('grp'), may hold values from 0 to 63, all different within a row; in each aligned block of 16 rows (0 to 15, 16 to 31, ...) at most 2 rows name the same one
- route_weights: int32 [1024, 4], P('grp'), may hold values from 1 to 65535
- w_gate_up: bfloat16 [64, 2880, 2880], P('grp', None, 'head'), may hold values from -0.109375 to 0.109375
- w_down: bfloat16 [64, 1440, 2880], P('grp', 'head'), may hold values from -0.15625 to 0.15625
Outputs:
- layer_out: bfloat16 [1024, 2880], P('grp', 'head')
Inputs may be any that keep to these rules, and one draw needn't show every extreme that they name: `route_ids`: in the 16 rows of one index of grp, at most 2 rows name the same expert; each row names 4 different experts.
All inputs are finite; a program needn't handle non-finite values.
Results may differ from a plain program's by a relative error of at most 0.025.
Values may be sent and summed in bfloat16 or wider, within the bound.
No kernel may reach another device: no remote copies, remote signals or barrier semaphores. Data moves between devices by JAX's collectives and lax.ppermute only.
A program may use at most 64 MiB of HBM per device.

v0:
```python
import jax
import jax.numpy as jnp
from jax import lax
from jax.sharding import PartitionSpec as P

epsilon = 1e-05
swish_alpha = 1.702


def cut_along(x, dim, devices):
    lengths = x.shape
    tiles = x.reshape(*lengths[:dim], devices, lengths[dim] // devices, *lengths[dim + 1 :])
    return jnp.moveaxis(tiles, dim, 0)


def summed_on_arrival(x, axis, dim):
    devices = lax.axis_size(axis)
    tiles = lax.all_to_all(cut_along(x, dim, devices), axis, 0, 0, tiled=True)
    return jnp.sum(tiles.astype(jnp.float32), axis=0)


def joined_along(tiles, dim):
    lengths = list(tiles.shape[1:])
    lengths[dim] *= tiles.shape[0]
    return jnp.moveaxis(tiles, 0, dim).reshape(lengths)


def from_everyone(x, axis):
    copies = jnp.broadcast_to(x, (lax.axis_size(axis), *x.shape))
    return lax.all_to_all(copies, axis, split_axis=0, concat_axis=0, tiled=True)


def gathered_copies(x, axis, dim):
    return joined_along(from_everyone(x, axis), dim)


def rms_norm(values, gain):
    as_float = values.astype(jnp.float32)
    mean_square = jnp.mean(as_float * as_float, axis=-1, keepdims=True)
    return (as_float * lax.rsqrt(mean_square + epsilon) * gain).astype(jnp.bfloat16)


def attend(queries, kv_cache, new_kv, positions, sink_logits):
    head_dim = new_kv.shape[2] // 2
    window = kv_cache.shape[2]
    row_count = queries.shape[0]
    kv_heads = queries.shape[1]
    groups = queries.shape[2] // head_dim
    slot_iota = jnp.arange(window, dtype=jnp.int32)
    current = positions % window
    slot_lag = (positions[:, None] - slot_iota[None, :]) % window
    is_valid = slot_lag <= positions[:, None]
    is_new = slot_iota[None, :] == current[:, None]
    merged = jnp.where(is_new[:, None, :, None], new_kv[:, :, None, :], kv_cache)
    key_part = merged[..., :head_dim]
    value_part = merged[..., head_dim:]
    query_part = queries.reshape(row_count, kv_heads, groups, head_dim)
    scores = jnp.einsum(
        "thgd,thwd->thgw", query_part, key_part, preferred_element_type=jnp.float32
    ) * head_dim ** (-0.5)
    scores = jnp.where(is_valid[:, None, None, :], scores, -jnp.inf)
    sink_col = sink_logits[None, :, :, None]
    largest = jnp.maximum(jnp.max(scores, axis=-1, keepdims=True), sink_col)
    weights_exp = jnp.exp(scores - largest)
    denominator = jnp.sum(weights_exp, axis=-1, keepdims=True) + jnp.exp(sink_col - largest)
    weights = (weights_exp / denominator).astype(jnp.bfloat16)
    mixed = jnp.einsum(
        "thgw,thwd->thgd", weights, value_part, preferred_element_type=jnp.float32
    ).astype(jnp.bfloat16)
    return mixed.reshape(row_count, kv_heads * groups * head_dim)


def local(
    residual,
    queries,
    kv_cache,
    new_kv,
    positions,
    sink_logits,
    out_proj,
    norm_gain,
    route_ids,
    route_weights,
    w_gate_up,
    w_down,
):
    row_count = residual.shape[0]
    width_all = out_proj.shape[2]
    share_width = width_all // lax.axis_size("head")
    share_start = lax.axis_index("head") * share_width
    mixed = attend(queries, kv_cache, new_kv, positions, sink_logits)
    partial_value = jnp.dot(
        mixed, out_proj.reshape(-1, width_all), preferred_element_type=jnp.float32
    )
    attention = summed_on_arrival(partial_value.astype(jnp.bfloat16), "head", 1)
    resid_here = lax.dynamic_slice_in_dim(residual, share_start, share_width, 1)
    hidden_here = (resid_here.astype(jnp.float32) + attention).astype(jnp.bfloat16)
    expert_count = lax.axis_size("grp")
    topk_count = route_ids.shape[1]
    capacity = max(2, row_count * topk_count // expert_count)
    flat_ids = route_ids.reshape(-1)
    assign_iota = jnp.arange(flat_ids.shape[0], dtype=jnp.int32)
    earlier = (flat_ids[:, None] == flat_ids[None, :]) & (
        assign_iota[:, None] > assign_iota[None, :]
    )
    slot_rank = jnp.sum(earlier.astype(jnp.int32), axis=1)
    slot_dest = flat_ids * capacity + slot_rank
    slot_iota = jnp.arange(expert_count * capacity, dtype=jnp.int32)
    send_table = (slot_iota[:, None] == slot_dest[None, :]).astype(jnp.bfloat16)
    take_table = (slot_dest[:, None] == slot_iota[None, :]).astype(jnp.float32)
    repeated = jnp.repeat(hidden_here, topk_count, axis=0)
    outgoing = jnp.dot(send_table, repeated, preferred_element_type=jnp.float32).astype(
        jnp.bfloat16
    )
    outgoing = outgoing.reshape(expert_count, capacity, -1)
    full_rows = gathered_copies(
        lax.all_to_all(outgoing, "grp", split_axis=0, concat_axis=0, tiled=True), "head", 2
    )
    normed = rms_norm(full_rows, norm_gain)
    item_lead = normed.shape[0]
    item_count = normed.shape[1]
    flat_rows = normed.reshape(item_lead * item_count, -1)
    projected = jnp.dot(flat_rows, w_gate_up[0], preferred_element_type=jnp.float32)
    pairs_view = projected.reshape(item_lead * item_count, -1, 2)
    gate_half = pairs_view[..., 0]
    up_half = pairs_view[..., 1]
    activated = ((up_half + 1.0) * gate_half * jax.nn.sigmoid(swish_alpha * gate_half)).astype(
        jnp.bfloat16
    )
    down_part = jnp.dot(activated, w_down[0], preferred_element_type=jnp.float32).reshape(
        item_lead, item_count, -1
    )
    summed = summed_on_arrival(down_part.astype(jnp.bfloat16), "head", 2)
    back_rows = lax.all_to_all(
        summed.astype(jnp.bfloat16), "grp", split_axis=0, concat_axis=0, tiled=True
    ).astype(summed.dtype)
    gathered = jnp.dot(
        take_table, back_rows.reshape(expert_count * capacity, -1), precision=lax.Precision.HIGHEST
    )
    weight_vec = route_weights.reshape(-1).astype(jnp.float32) / 65536.0
    mixture = jnp.sum((gathered * weight_vec[:, None]).reshape(row_count, topk_count, -1), axis=1)
    return (hidden_here.astype(jnp.float32) + mixture).astype(jnp.bfloat16)


def solution(mesh):
    in_specs = (
        P("grp", None),
        P("grp", "head", None),
        P("grp", "head", None, None),
        P("grp", "head", None),
        P("grp"),
        P("head", None),
        P("head", None, None),
        P(),
        P("grp", None),
        P("grp", None),
        P("grp", None, "head"),
        P("grp", "head", None),
    )
    out_specs = P("grp", "head")
    return jax.shard_map(local, mesh=mesh, in_specs=in_specs, out_specs=out_specs, check_vma=False)
```

profile of v0, /device:TPU:2, one launch (start us, length us, event | category | flops | bytes accessed | tf_op | source)
XLA Modules:
  0.0 117.2 jit_solution(15492725431922988255)
XLA Ops:
  0.0 0.8 and_select_fusion
  0.8 0.7 fusion.22
  1.5 1.3 %copy.79 = bf16[16,1,128,128]{2,3,0,1:T(8,128)(2,1)S(1)} copy(bf16[16,1,128,128]{3,2,1,0:T(8,128)(2,1)} %param.14) | data formatting | bytes 1048576 | tf_op args[2]
  2.9 0.8 reshape.240
  3.7 1.0 broadcast_select_fusion
  7.0 4.5 %all-to-all-start = ((bf16[8,16,360]{2,1,0:T(8,128)(2,1)}), bf16[8,16,360]{2,1,0:T(8,128)(2,1)S(1)}, u32[]{:S(2)}, u32[]{:S(2)}) async-start(bf16[8,16,360]{2,1,0:T(8,128)(2,1)} %bitcast.44), calls=%async_computation | async-start | bytes 196608 | tf_op jit(solution)/shard_map/all_to_all | solution.py:18
  11.8 5.4 %all-to-all-done = bf16[8,16,360]{2,1,0:T(8,128)(2,1)S(1)} async-done(((bf16[8,16,360]{2,1,0:T(8,128)(2,1)}), bf16[8,16,360]{2,1,0:T(8,128)(2,1)S(1)}, u32[]{:S(2)}, u32[]{:S(2)}) %all-to-all-start) | async-done | bytes 92192 | tf_op jit(solution)/shard_map/all_to_all | solution.py:18
  17.3 0.8 add_convert_fusion.1
  18.6 33.6 %all_to_all.25 = bf16[64,2,360]{2,1,0:T(2,128)(2,1)S(1)} all-to-all(bf16[64,2,360]{2,1,0:T(2,128)(2,1)S(1)} %reshape.247), channel_id=1, replica_groups=mesh['grp'=64,'head'=8] {'grp'}, dimensions={0} | all-to-all | bytes 184320 | tf_op jit(solution)/shard_map/all_to_all | solution.py:117
  52.2 1.3 %broadcast_in_dim.40 = bf16[8,64,2,360]{3,2,1,0:T(2,128)(2,1)} broadcast(bf16[64,2,360]{2,1,0:T(2,128)(2,1)S(1)} %all_to_all.25), dimensions={1,2,3} | broadcast | bytes 829440 | tf_op jit(solution)/shard_map/broadcast_in_dim | solution.py:29
  53.5 3.5 %all-to-all-start.2 = ((bf16[8,64,2,360]{3,2,1,0:T(2,128)(2,1)}), bf16[8,64,2,360]{3,2,1,0:T(2,128)(2,1)S(1)}, u32[]{:S(2)}, u32[]{:S(2)}) async-start(bf16[8,64,2,360]{3,2,1,0:T(2,128)(2,1)} %broadcast_in_dim.40), calls=%async_computation.2 | async-start | bytes 1572864 | tf_op jit(solution)/shard_map/all_to_all | solution.py:30
  57.2 5.2 %dot_general.30 = bf16[180,2,2880]{2,1,0:T(2,128)(2,1)} reshape(bf16[360,2880]{1,0:T(8,128)(2,1)} %bitcast.46) | data formatting | bytes 4147200 | tf_op jit(solution)/shard_map/dot_general | solution.py:123
  62.4 7.7 %all-to-all-done.2 = bf16[8,64,2,360]{3,2,1,0:T(2,128)(2,1)S(1)} async-done(((bf16[8,64,2,360]{3,2,1,0:T(2,128)(2,1)}), bf16[8,64,2,360]{3,2,1,0:T(2,128)(2,1)S(1)}, u32[]{:S(2)}, u32[]{:S(2)}) %all-to-all-start.2) | async-done | bytes 737312 | tf_op jit(solution)/shard_map/all_to_all | solution.py:30
  70.1 1.0 fusion.2
  71.1 1.0 fusion.9
  72.1 0.9 copy.85
  73.0 0.6 convert_element_type.84
  73.6 2.3 %fusion = f32[128,180,2]{0,1,2:T(8,128)S(1)} fusion(bf16[180,2,2880]{2,1,0:T(2,128)(2,1)} %dot_general.30, bf16[128,2880]{1,0:T(8,128)(2,1)S(1)} %convert_element_type.84), kind=kOutput, calls=%fused_computation.2 | convolution fusion | flops 265420800 | bytes 2995200 | tf_op jit(solution)/shard_map/dot_general | solution.py:123
  76.2 1.6 %convolution_convert_fusion = bf16[64,2,2880]{2,0,1:T(8,128)(2,1)S(1)} fusion(bf16[1,180,2880]{2,1,0:T(8,128)(2,1)} %param.23, bf16[64,2,180]{2,1,0:T(2,128)(2,1)S(1)} %convert_element_type.86), kind=kOutput, calls=%fused_computation | convolution fusion | flops 133079040 | bytes 1820160 | tf_op jit(solution)/shard_map/dot_general | solution.py:130
  77.8 1.1 reshape.248
  79.0 15.6 %all_to_all.26 = bf16[8,64,2,360]{3,1,2,0:T(8,128)(2,1)S(1)} all-to-all(bf16[8,64,2,360]{3,1,2,0:T(8,128)(2,1)S(1)} %bitcast.45), channel_id=1, replica_groups=mesh['grp'=64,'head'=8] {'head'}, dimensions={0} | all-to-all | bytes 1474560 | tf_op jit(solution)/shard_map/all_to_all | solution.py:18
  94.7 0.7 copy.92
  95.4 5.5 %all-to-all-start.4 = ((bf16[64,2,360]{2,1,0:T(2,128)(2,1)}), bf16[64,2,360]{2,1,0:T(2,128)(2,1)S(1)}, u32[]{:S(2)}, u32[]{:S(2)}) async-start(bf16[64,2,360]{2,1,0:T(2,128)(2,1)} %copy.92), calls=%async_computation.4 | async-start | bytes 196608 | tf_op jit(solution)/shard_map/all_to_all | solution.py:134
  101.1 15.1 %all-to-all-done.4 = bf16[64,2,360]{2,1,0:T(2,128)(2,1)S(1)} async-done(((bf16[64,2,360]{2,1,0:T(2,128)(2,1)}), bf16[64,2,360]{2,1,0:T(2,128)(2,1)S(1)}, u32[]{:S(2)}, u32[]{:S(2)}) %all-to-all-start.4) | async-done | bytes 92192 | tf_op jit(solution)/shard_map/all_to_all | solution.py:134
  (45 shorter events, 4.8 us)
Async XLA Ops:
  0.0 5.6 %copy-start = (bf16[1,256,2880]{1,2,0:T(8,128)(2,1)S(1)}, bf16[1,256,2880]{1,2,0:T(8,128)(2,1)}, u32[]{:S(2)}) copy-start(bf16[1,256,2880]{1,2,0:T(8,128)(2,1)} %param.18) | copy-start | bytes 4423684
  0.0 5.0 %copy-start.3 = (f32[1,4]{1,0:T(1,128)S(1)}, f32[1,4]{1,0:T(1,128)}, u32[]{:S(2)}) copy-start(f32[1,4]{1,0:T(1,128)} %param.17) | copy-start | bytes 52
  4.7 6.7 %copy-start.2 = (s32[16,4]{0,1:T(4,128)S(1)}, s32[16,4]{0,1:T(4,128)}, u32[]{:S(2)}) copy-start(s32[16,4]{0,1:T(4,128)} %param.20) | copy-start | bytes 772
  7.0 10.3 %all-to-all-start = ((bf16[8,16,360]{2,1,0:T(8,128)(2,1)}), bf16[8,16,360]{2,1,0:T(8,128)(2,1)S(1)}, u32[]{:S(2)}, u32[]{:S(2)}) async-start(bf16[8,16,360]{2,1,0:T(8,128)(2,1)} %bitcast.44), calls=%async_computation | async-start | bytes 196608 | tf_op jit(solution)/shard_map/all_to_all | solution.py:18
  18.1 39.0 %copy-start.1 = (f32[2880]{0:T(1024)S(1)}, f32[2880]{0:T(1024)}, u32[]{:S(2)}) copy-start(f32[2880]{0:T(1024)} %param.19) | copy-start | bytes 34564
  53.5 16.6 %all-to-all-start.2 = ((bf16[8,64,2,360]{3,2,1,0:T(2,128)(2,1)}), bf16[8,64,2,360]{3,2,1,0:T(2,128)(2,1)S(1)}, u32[]{:S(2)}, u32[]{:S(2)}) async-start(bf16[8,64,2,360]{3,2,1,0:T(2,128)(2,1)} %broadcast_in_dim.40), calls=%async_computation.2 | async-start | bytes 1572864 | tf_op jit(solution)/shard_map/all_to_all | solution.py:30
  79.0 21.9 %copy-start.4 = (s32[16,4]{0,1:T(4,128)S(1)}, s32[16,4]{0,1:T(4,128)}, u32[]{:S(2)}) copy-start(s32[16,4]{0,1:T(4,128)} %param.21) | copy-start | bytes 772
  95.4 20.7 %all-to-all-start.4 = ((bf16[64,2,360]{2,1,0:T(2,128)(2,1)}), bf16[64,2,360]{2,1,0:T(2,128)(2,1)S(1)}, u32[]{:S(2)}, u32[]{:S(2)}) async-start(bf16[64,2,360]{2,1,0:T(2,128)(2,1)} %copy.92), calls=%async_computation.4 | async-start | bytes 196608 | tf_op jit(solution)/shard_map/all_to_all | solution.py:134
where the time goes:
time: 118 us; the launch traced here: 117 us
  blocking collectives  49.2 us (42%)
  waiting for transfers between devices  28.2 us (24%)
  local copies, waits for them, and re-layouts  13.9 us (12%)
  starting transfers between devices  13.5 us (11%)
  other arithmetic  6.6 us (6%)
  matrix products  5.47 us (5%)
    all_to_all x1, blocking collectives, local(): lax.all_to_all(outgoing, 'grp', split_axis=0, concat_axis=0, tiled=True)  33.6 us
    all_to_all x1, blocking collectives, summed_on_arrival(): tiles = lax.all_to_all(cut_along(x, dim, devices), axis, 0, 0, tiled=True)  15.6 us
    all_to_all x1, waiting for transfers between devices, local(): lax.all_to_all(summed.astype(jnp.bfloat16), 'grp', split_axis=0, concat_a...  15.1 us
    all_to_all x1, waiting for transfers between devices, from_everyone(): return lax.all_to_all(copies, axis, split_axis=0, concat_axis=0, tiled=True)  7.71 us
    all_to_all x1, starting transfers between devices, local(): lax.all_to_all(summed.astype(jnp.bfloat16), 'grp', split_axis=0, concat_a...  5.46 us
    all_to_all x1, waiting for transfers between devices, summed_on_arrival(): tiles = lax.all_to_all(cut_along(x, dim, devices), axis, 0, 0, tiled=True)  5.42 us
    dot_general x1, local copies, waits for them, and re-layouts, local(): jnp.dot(flat_rows, w_gate_up[0], preferred_element_type=jnp.float32)  5.24 us
    all_to_all x1, starting transfers between devices, summed_on_arrival(): tiles = lax.all_to_all(cut_along(x, dim, devices), axis, 0, 0, tiled=True)  4.47 us
  transfers between devices with their start and end apart: 3, of which 3 were waited for; matrix products, arithmetic and copies ran while one was open for 5% of the time, Pallas kernels for 0%

commit v1 on v0

v1 whole, which is shorter than its diff:
```python
import functools

import jax
import jax.numpy as jnp
from jax import lax
from jax.experimental import pallas as pl
from jax.experimental.pallas import tpu as pltpu
from jax.sharding import Mesh, PartitionSpec as P

epsilon = 1e-05
swish_alpha = 1.702

GRID = (16, 4, 4, 2)
GRP = ("z", "x")
HEAD = ("y", "core")
MIB = 1 << 20
KV_PIECES = 4


def attend_kernel(
    pos_hbm,
    sink_hbm,
    q_hbm,
    kv_hbm,
    new_hbm,
    proj_hbm,
    out_ref,
    pos_ref,
    sink_ref,
    q_ref,
    kv_ref,
    new_ref,
    proj_ref,
    sems,
):
    rows, window, width = kv_ref.shape
    piece = rows // KV_PIECES
    copies = [
        pltpu.make_async_copy(src, dst, sems.at[i])
        for i, (src, dst) in enumerate(
            [(q_hbm, q_ref), (new_hbm, new_ref), (pos_hbm, pos_ref), (sink_hbm, sink_ref)]
        )
    ]
    kv_copies = [
        pltpu.make_async_copy(
            kv_hbm.at[pl.ds(i * piece, piece)], kv_ref.at[pl.ds(i * piece, piece)], sems.at[4 + i]
        )
        for i in range(KV_PIECES)
    ]
    proj_copy = pltpu.make_async_copy(proj_hbm, proj_ref, sems.at[4 + KV_PIECES])
    for copy in copies + kv_copies:
        copy.start()
    proj_copy.start()
    for copy in copies:
        copy.wait()
    half = width // 2
    groups = 4
    shares, _, share_width = out_ref.shape
    lane = lax.broadcasted_iota(jnp.int32, (rows, width), 1)
    row = lax.broadcasted_iota(jnp.int32, (rows, width), 0)
    low = lane < half
    q = q_ref[...].astype(jnp.float32)
    parts = []
    for pair in range(groups // 2):
        both = q[:, pair * width : (pair + 1) * width]
        parts.append(jnp.where(low, both, 0.0))
        parts.append(jnp.where(low, pltpu.roll(both, half, 1), 0.0))
    stacked = jnp.concatenate(parts, axis=0)
    stacked_low = stacked.astype(jnp.bfloat16)
    new = new_ref[...].astype(jnp.float32)
    new_all = jnp.concatenate([new] * groups, axis=0)

    pos = jnp.zeros((rows, width), jnp.int32)
    for t in range(rows):
        pos = jnp.where(row == t, pos_ref[t], pos)
    pos = jnp.concatenate([pos] * groups, axis=0)
    lanes = lax.broadcasted_iota(jnp.int32, pos.shape, 1)
    request = lax.broadcasted_iota(jnp.int32, pos.shape, 0) % rows
    group = lax.broadcasted_iota(jnp.int32, (groups * rows, 1), 0) // rows
    sink = jnp.zeros((groups * rows, 1), jnp.float32)
    for g in range(groups):
        sink = jnp.where(group == g, sink_ref[0, g], sink)

    scores = jnp.zeros((groups * rows, window), jnp.float32)
    for t in range(rows):
        if t % piece == 0:
            kv_copies[t // piece].wait()
        found = lax.dot_general(
            stacked_low, kv_ref[t], (((1,), (1,)), ((), ())), preferred_element_type=jnp.float32
        )
        scores = jnp.where(request == t, found, scores)
    newest = jnp.sum(stacked * new_all, axis=1, keepdims=True)
    is_new = lanes == (pos & (window - 1))
    scores = jnp.where(is_new, newest, scores) * (half**-0.5)
    scores = jnp.where(lanes <= pos, scores, -jnp.inf)
    largest = jnp.maximum(jnp.max(scores, axis=1, keepdims=True), sink)
    raised = jnp.exp(scores - largest)
    total = jnp.sum(raised, axis=1, keepdims=True) + jnp.exp(sink - largest)
    weights = (raised / total).astype(jnp.bfloat16).astype(jnp.float32)
    newest_weight = jnp.sum(jnp.where(is_new, weights, 0.0), axis=1, keepdims=True)
    older = jnp.where(is_new, 0.0, weights).astype(jnp.bfloat16)
    mixed = jnp.zeros((groups * rows, width), jnp.float32)
    for t in range(rows):
        found = jnp.dot(older, kv_ref[t], preferred_element_type=jnp.float32)
        mixed = jnp.where(request == t, found, mixed)
    mixed = mixed + newest_weight * new_all
    merged = []
    for pair in range(groups // 2):
        first = mixed[2 * pair * rows : (2 * pair + 1) * rows]
        second = mixed[(2 * pair + 1) * rows : (2 * pair + 2) * rows]
        merged.append(jnp.where(low, pltpu.roll(first, half, 1), second))
    merged = jnp.concatenate(merged, axis=1).astype(jnp.bfloat16)
    proj_copy.wait()
    for s in range(shares):
        out_ref[s] = lax.dot_general(
            merged,
            proj_ref[pl.ds(s * share_width, share_width), :],
            (((1,), (1,)), ((), ())),
            preferred_element_type=jnp.float32,
        ).astype(jnp.bfloat16)


def attend(positions, sink_logits, queries, kv_cache, new_kv, out_proj):
    rows, _, window, width = kv_cache.shape
    features = out_proj.shape[2]
    hbm = pl.BlockSpec(memory_space=pltpu.HBM)
    return pl.pallas_call(
        attend_kernel,
        out_shape=jax.ShapeDtypeStruct((8, rows, features // 8), jnp.bfloat16),
        in_specs=[hbm] * 6,
        out_specs=pl.BlockSpec(memory_space=pltpu.VMEM),
        scratch_shapes=[
            pltpu.SMEM((rows,), jnp.int32),
            pltpu.SMEM(sink_logits.shape, jnp.float32),
            pltpu.VMEM((rows, queries.shape[2]), jnp.bfloat16),
            pltpu.VMEM((rows, window, width), jnp.bfloat16),
            pltpu.VMEM((rows, width), jnp.bfloat16),
            pltpu.VMEM((features, out_proj.shape[1]), jnp.bfloat16),
            pltpu.SemaphoreType.DMA((5 + KV_PIECES,)),
        ],
        compiler_params=pltpu.CompilerParams(vmem_limit_bytes=8 * MIB),
        name="attend",
    )(
        *(
            pltpu.with_memory_space_constraint(x, pltpu.HBM)
            for x in (
                positions,
                sink_logits,
                queries.reshape(rows, -1),
                kv_cache.reshape(rows, window, width),
                new_kv.reshape(rows, width),
                jnp.swapaxes(out_proj[0], 0, 1),
            )
        )
    )


def up_kernel(core_ref, x_ref, w_ref, down_ref, act_ref, send_ref, held_ref):
    other = 1 - core_ref[0]
    x = x_ref[...]
    wide = x.astype(jnp.float32)
    mean_square = jnp.mean(wide * wide, axis=0, keepdims=True)
    projected = jnp.dot(w_ref[...], x, preferred_element_type=jnp.float32)
    held_ref[...] = projected * lax.rsqrt(mean_square + epsilon)
    hidden_units = held_ref.shape[0] // 2
    gate = held_ref[pl.ds(0, hidden_units, stride=2), :]
    up = held_ref[pl.ds(1, hidden_units, stride=2), :]
    act = ((up + 1.0) * gate * jax.nn.sigmoid(swish_alpha * gate)).astype(jnp.bfloat16)
    act_ref[...] = act
    send_ref[...] = jnp.dot(
        down_ref[other], act, preferred_element_type=jnp.float32
    ).astype(jnp.bfloat16)


def down_kernel(core_ref, act_ref, down_ref, out_ref):
    out_ref[...] = jnp.dot(
        down_ref[core_ref[0]], act_ref[...], preferred_element_type=jnp.float32
    )


def local(
    residual,
    queries,
    kv_cache,
    new_kv,
    positions,
    sink_logits,
    out_proj,
    norm_gain,
    route_ids,
    route_weights,
    w_gate_up,
    w_down,
):
    rows, features = residual.shape
    experts = lax.axis_size(GRP)
    shares = lax.axis_size(HEAD)
    y_size = lax.axis_size("y")
    share = features // shares
    topk = route_ids.shape[1]
    capacity = 2
    slots = experts * capacity
    units = w_down.shape[1]
    core = lax.axis_index("core").astype(jnp.int32).reshape(1)
    vmem = pl.BlockSpec(memory_space=pltpu.VMEM)
    smem = pl.BlockSpec(memory_space=pltpu.SMEM)

    parts = attend(positions, sink_logits, queries, kv_cache, new_kv, out_proj)
    parts = lax.all_to_all(parts, HEAD, 0, 0, tiled=True)
    attention = jnp.sum(parts.astype(jnp.float32), axis=0)
    resid_here = lax.optimization_barrier(
        lax.dynamic_slice_in_dim(residual, lax.axis_index(HEAD) * share, share, 1)
    )
    hidden = (resid_here.astype(jnp.float32) + attention).astype(jnp.bfloat16)

    flat_ids = route_ids.reshape(-1)
    order = jnp.arange(rows * topk, dtype=jnp.int32)
    earlier = (flat_ids[:, None] == flat_ids[None, :]) & (order[:, None] > order[None, :])
    slot = (flat_ids * capacity + jnp.sum(earlier.astype(jnp.int32), axis=1)).reshape(rows, topk)
    hit = slot[:, :, None] == jnp.arange(slots, dtype=jnp.int32)[None, None, :]
    scale = route_weights.astype(jnp.float32) / 65536.0
    pick, combine = lax.optimization_barrier(
        (
            jnp.sum(hit.astype(jnp.float32), axis=1).astype(jnp.bfloat16),
            jnp.sum(jnp.where(hit, scale[:, :, None], 0.0), axis=1),
        )
    )

    gate_up = (
        jnp.swapaxes(w_gate_up[0], 0, 1).astype(jnp.float32) * norm_gain[None, :]
    ).astype(jnp.bfloat16)
    down = (
        w_down[0].reshape(units, y_size, 2, share).transpose(2, 1, 3, 0).reshape(2, -1, units)
    )

    outgoing = lax.dot_general(
        pick, hidden, (((0,), (0,)), ((), ())), preferred_element_type=jnp.float32
    ).astype(jnp.bfloat16)
    got = lax.all_to_all(outgoing.reshape(experts, capacity, share), GRP, 0, 0, tiled=True)
    got, gate_up, down = lax.optimization_barrier((got, gate_up, down))
    got = jnp.swapaxes(got.reshape(slots, share), 0, 1)
    mine = lax.all_to_all(
        jnp.broadcast_to(got[None], (y_size, share, slots)), "y", 0, 0, tiled=True
    )
    swap = [(0, 1), (1, 0)]
    theirs = lax.ppermute(mine, "core", swap)
    is_low = core[0] == 0
    full = jnp.stack(
        [jnp.where(is_low, mine, theirs), jnp.where(is_low, theirs, mine)], axis=1
    ).reshape(features, slots)

    act, sent = pl.pallas_call(
        up_kernel,
        out_shape=(
            jax.ShapeDtypeStruct((units, slots), jnp.bfloat16),
            jax.ShapeDtypeStruct((y_size * share, slots), jnp.bfloat16),
        ),
        in_specs=[smem, vmem, vmem, vmem],
        out_specs=(vmem, vmem),
        scratch_shapes=[pltpu.VMEM((2 * units, slots), jnp.float32)],
        compiler_params=pltpu.CompilerParams(vmem_limit_bytes=12 * MIB),
        name="up",
    )(core, full, gate_up, down)
    arrived = lax.ppermute(sent, "core", swap)
    own = pl.pallas_call(
        down_kernel,
        out_shape=jax.ShapeDtypeStruct((y_size * share, slots), jnp.float32),
        in_specs=[smem, vmem, vmem],
        out_specs=vmem,
        compiler_params=pltpu.CompilerParams(vmem_limit_bytes=12 * MIB),
        name="down",
    )(core, act, down)
    paired = (own + arrived.astype(jnp.float32)).astype(jnp.bfloat16)
    paired = lax.all_to_all(paired.reshape(y_size, share, slots), "y", 0, 0, tiled=True)
    summed = jnp.sum(paired.astype(jnp.float32), axis=0).astype(jnp.bfloat16)
    back = lax.all_to_all(
        jnp.swapaxes(summed, 0, 1).reshape(experts, capacity, share), GRP, 0, 0, tiled=True
    )
    mixture = jnp.dot(
        combine,
        back.reshape(slots, share).astype(jnp.float32),
        precision=lax.Precision.HIGHEST,
    )
    return (hidden.astype(jnp.float32) + mixture).astype(jnp.bfloat16)


def solution(mesh):
    fine = Mesh(mesh.devices.reshape(GRID), ("z", "x", "y", "core"))
    in_specs = (
        P(GRP, None),
        P(GRP, HEAD, None),
        P(GRP, HEAD, None, None),
        P(GRP, HEAD, None),
        P(GRP),
        P(HEAD, None),
        P(HEAD, None, None),
        P(),
        P(GRP, None),
        P(GRP, None),
        P(GRP, None, HEAD),
        P(GRP, HEAD, None),
    )
    return jax.shard_map(
        local, mesh=fine, in_specs=in_specs, out_specs=P(GRP, HEAD), check_vma=False
    )
```

time: 118 us -> 102 us (0.86)
  starting transfers between devices: 13.5 us -> 27.2 us
  waiting for transfers between devices: 28.2 us -> 15.3 us
  blocking collectives: 49.2 us -> 42.9 us
  local copies, waits for them, and re-layouts: 13.9 us -> 7.62 us
  Pallas kernels: 0 us -> 5.44 us
  matrix products: 5.47 us -> 1.02 us
  other arithmetic: 6.6 us -> 2.28 us
    all_to_all x3 -> x2, waiting for transfers between devices: 28.2 us -> 12.7 us  [the longest x1 7.63 us: local(): lax.all_to_all(outgoing.reshape(experts, capacity, share), GRP, 0, 0, til...]
    all_to_all x3 -> x2, starting transfers between devices: 13.5 us -> 23.1 us  [the longest x1 18.6 us: local(): lax.all_to_all(outgoing.reshape(experts, capacity, share), GRP, 0, 0, til...]
    all_to_all x2 -> x3, blocking collectives: 49.2 us -> 42.9 us  [the longest x1 22.4 us: local(): lax.all_to_all(jnp.swapaxes(summed, 0, 1).reshape(experts, capacity, shar...]
    pallas_call x0 -> x3, Pallas kernels: none -> 5.44 us  [the longest x1 3.6 us: attend(): pl.pallas_call(attend_kernel, out_shape=jax.ShapeDtypeStruct((8, rows, fe...]
    dot_general x1 -> x0, local copies, waits for them, and re-layouts: 5.24 us -> none  [local(): jnp.dot(flat_rows, w_gate_up[0], preferred_element_type=jnp.float32)]
    another operation x1 -> x2, local copies, waits for them, and re-layouts: 0.78 us -> 5.81 us  [local(): w_down[0].reshape(units, y_size, 2, share).transpose(2, 1, 3, 0)]
    dot_general x7 -> x2, matrix products: 5.47 us -> 1.02 us  [the longest x1 0.77 us: local(): jnp.dot(combine, back.reshape(slots, share).astype(jnp.float32), precisio...]
    ppermute x0 -> x2, starting transfers between devices: none -> 4.12 us  [the longest x1 2.21 us: local(): arrived = lax.ppermute(sent, 'core', swap)]
  transfers between devices with their start and end apart: 3 -> 4, of which waited for: 3 -> 4; matrix products, arithmetic and copies ran while one was open for 5% -> 8% of each run, Pallas kernels for 0% -> 0%
where the time goes in v1:
time: 102 us
  blocking collectives  42.9 us (42%)
  starting transfers between devices  27.2 us (27%)
  waiting for transfers between devices  15.3 us (15%)
  local copies, waits for them, and re-layouts  7.62 us (7%)
  Pallas kernels  5.44 us (5%)
  other arithmetic  2.28 us (2%)
  matrix products  1.02 us (1%)
    all_to_all x1, blocking collectives, local(): lax.all_to_all(jnp.swapaxes(summed, 0, 1).reshape(experts, capacity, shar...  22.4 us
    all_to_all x1, starting transfers between devices, local(): lax.all_to_all(outgoing.reshape(experts, capacity, share), GRP, 0, 0, til...  18.6 us
    all_to_all x1, blocking collectives, local(): lax.all_to_all(paired.reshape(y_size, share, slots), 'y', 0, 0, tiled=True)  10.9 us
    all_to_all x1, blocking collectives, local(): lax.all_to_all(jnp.broadcast_to(got[None], (y_size, share, slots)), 'y',...  9.63 us
    all_to_all x1, waiting for transfers between devices, local(): lax.all_to_all(outgoing.reshape(experts, capacity, share), GRP, 0, 0, til...  7.63 us
    another operation x2, local copies, waits for them, and re-layouts, local(): w_down[0].reshape(units, y_size, 2, share).transpose(2, 1, 3, 0)  5.81 us
    all_to_all x1, waiting for transfers between devices, local(): parts = lax.all_to_all(parts, HEAD, 0, 0, tiled=True)  5.03 us
    all_to_all x1, starting transfers between devices, local(): parts = lax.all_to_all(parts, HEAD, 0, 0, tiled=True)  4.48 us
  transfers between devices with their start and end apart: 4, of which 4 were waited for; matrix products, arithmetic and copies ran while one was open for 8% of the time, Pallas kernels for 0%

profile of v1, /device:TPU:2, one launch (start us, length us, event | category | flops | bytes accessed | tf_op | source)
XLA Modules:
  0.0 102.1 jit_solution(5203608736656318811)
XLA Ops:
  0.0 3.6 %attend.1 = bf16[8,16,360]{2,1,0:T(8,128)(2,1)} custom-call(s32[16]{0:T(128)} %pos_hbm.1, f32[1,4]{1,0:T(1,128)} %sink_hbm.1, bf16[16,256]{1,0:T(8,128)(2,1)} %bitcast.36, bf16[16,128,128]{2,1,0:T(8,128)(2,1)} %bitcast.33, bf16[16,128]{1,0:T(8,128)(2,1)} %bitcast.37, bf16[2880,256]{1,0:T(8,128)(2,1)} %bitcast.31), custom_call_target="tpu_custom_call" | custom-call | tf_op jit(solution)/shard_map/attend/pallas_call | solution.py:127
  3.6 4.5 %all-to-all-start = ((bf16[8,16,360]{2,1,0:T(8,128)(2,1)}), bf16[8,16,360]{2,1,0:T(8,128)(2,1)S(1)}, u32[]{:S(2)}, u32[]{:S(2)}) async-start(bf16[8,16,360]{2,1,0:T(8,128)(2,1)} %attend.1), calls=%async_computation | async-start | bytes 196608 | tf_op jit(solution)/shard_map/all_to_all | solution.py:209
  8.3 0.2 convert_reduce_fusion.2
  8.9 5.0 %all-to-all-done = bf16[8,16,360]{2,1,0:T(8,128)(2,1)S(1)} async-done(((bf16[8,16,360]{2,1,0:T(8,128)(2,1)}), bf16[8,16,360]{2,1,0:T(8,128)(2,1)S(1)}, u32[]{:S(2)}, u32[]{:S(2)}) %all-to-all-start) | async-done | bytes 92192 | tf_op jit(solution)/shard_map/all_to_all | solution.py:209
  13.9 0.2 convolution_convert_fusion
  14.2 0.1 copy.43
  14.3 0.7 reshape.51
  15.0 18.6 %all-to-all-start.1 = ((bf16[64,2,360]{2,1,0:T(2,128)(2,1)}), bf16[64,2,360]{2,1,0:T(2,128)(2,1)S(1)}, u32[]{:S(2)}, u32[]{:S(2)}) async-start(bf16[64,2,360]{2,1,0:T(2,128)(2,1)} %reshape.51), calls=%async_computation.1 | async-start | bytes 196608 | tf_op jit(solution)/shard_map/all_to_all | solution.py:239
  33.7 1.7 %fusion.1.w_ref = bf16[360,2880]{1,0:T(8,128)(2,1)} fusion(bf16[1,2880,360]{1,2,0:T(8,128)(2,1)S(1)} %copy-done.2, f32[2880]{0:T(1024)S(1)} %copy-done.3), kind=kLoop, calls=%fused_computation.2 | loop fusion | flops 3110400 | bytes 4158720 | tf_op jit(solution)/shard_map/convert_element_type | solution.py:231
  35.4 4.6 %reshape_squeeze.3 = bf16[180,4,2,360]{3,2,1,0:T(2,128)(2,1)S(1)} reshape(bf16[1,180,2880]{2,1,0:T(8,128)(2,1)} %param.23) | data formatting | bytes 2073600 | tf_op jit(solution)/shard_map/reshape;squeeze | solution.py:233
  40.1 1.2 %copy.44 = bf16[180,4,2,360]{0,3,1,2:T(8,128)(2,1)S(1)} copy(bf16[180,4,2,360]{3,2,1,0:T(2,128)(2,1)S(1)} %reshape_squeeze.3) | data formatting | bytes 2073600 | tf_op jit(solution)/shard_map/reshape;squeeze | solution.py:233
  41.2 7.6 %all-to-all-done.1 = bf16[64,2,360]{2,1,0:T(2,128)(2,1)S(1)} async-done(((bf16[64,2,360]{2,1,0:T(2,128)(2,1)}), bf16[64,2,360]{2,1,0:T(2,128)(2,1)S(1)}, u32[]{:S(2)}, u32[]{:S(2)}) %all-to-all-start.1) | async-done | bytes 92192 | tf_op jit(solution)/shard_map/all_to_all | solution.py:239
  49.0 0.1 copy.45
  49.1 9.6 %all_to_all.25 = bf16[4,360,128]{2,1,0:T(8,128)(2,1)S(1)} all-to-all(bf16[4,360,128]{2,1,0:T(8,128)(2,1)S(1)} %broadcast_in_dim.16), channel_id=1, replica_groups=mesh['z'=16,'x'=4,'y'=4,'core'=2] {'y'}, dimensions={0} | all-to-all | bytes 737280 | tf_op jit(solution)/shard_map/all_to_all | solution.py:242
  58.8 1.9 %collective-permute-start = (bf16[4,360,128]{2,1,0:T(8,128)(2,1)S(1)}, bf16[4,360,128]{2,1,0:T(8,128)(2,1)S(1)}, u32[]{:S(2)}, u32[]{:S(2)}) collective-permute-start(bf16[4,360,128]{2,1,0:T(8,128)(2,1)S(1)} %all_to_all.25), channel_id=1, source_target_pairs={{0,1},{1,0},{2,3},{3,2},{4,5},{5,4},{6,7},{7,6},{8,9},{9,8},{10,11... | collective-permute-start | bytes 1105928 | tf_op jit(solution)/shard_map/ppermute | solution.py:246
  60.7 1.6 %collective-permute-done = bf16[4,360,128]{2,1,0:T(8,128)(2,1)S(1)} collective-permute-done((bf16[4,360,128]{2,1,0:T(8,128)(2,1)S(1)}, bf16[4,360,128]{2,1,0:T(8,128)(2,1)S(1)}, u32[]{:S(2)}, u32[]{:S(2)}) %collective-permute-start) | collective-permute-done | bytes 368672 | tf_op jit(solution)/shard_map/ppermute | solution.py:246
  62.5 1.5 %up.1 = (bf16[180,128]{1,0:T(8,128)(2,1)S(1)}, bf16[1440,128]{1,0:T(8,128)(2,1)S(1)}) custom-call(s32[1]{0:T(128)} %bitcast.5.core_ref, bf16[2880,128]{1,0:T(8,128)(2,1)S(1)} %bitcast.30, bf16[360,2880]{1,0:T(8,128)(2,1)S(1)} %copy-done.1, bf16[2,1440,180]{2,1,0:T(8,128)(2,1)S(1)} %bitcast.28), custom_call_target="tpu_custom_call" | custom-call | tf_op jit(solution)/shard_map/up/pallas_call | solution.py:252
  64.0 2.2 %collective-permute-start.1 = (bf16[1440,128]{1,0:T(8,128)(2,1)S(1)}, bf16[1440,128]{1,0:T(8,128)(2,1)S(1)}, u32[]{:S(2)}, u32[]{:S(2)}) collective-permute-start(bf16[1440,128]{1,0:T(8,128)(2,1)S(1)} %get-tuple-element.18), channel_id=1, source_target_pairs={{0,1},{1,0},{2,3},{3,2},{4,5},{5,4},{6,7},{7,6},{8,9},{9,8},{10,11... | collective-permute-start | bytes 1105928 | tf_op jit(solution)/shard_map/ppermute | solution.py:264
  66.2 0.3 down.1
  66.6 1.0 collective-permute-done.1
  67.7 10.9 %all_to_all.26 = bf16[4,360,128]{2,1,0:T(8,128)(2,1)S(1)} all-to-all(bf16[4,360,128]{2,1,0:T(8,128)(2,1)S(1)} %bitcast.32), channel_id=1, replica_groups=mesh['z'=16,'x'=4,'y'=4,'core'=2] {'y'}, dimensions={0} | all-to-all | bytes 737280 | tf_op jit(solution)/shard_map/all_to_all | solution.py:274
  78.7 0.1 copy.47
  78.9 22.4 %all_to_all.27 = bf16[64,2,360]{2,1,0:T(2,128)(2,1)S(1)} all-to-all(bf16[64,2,360]{2,1,0:T(2,128)(2,1)S(1)} %reshape.56), channel_id=1, replica_groups=mesh['z'=16,'x'=4,'y'=4,'core'=2] {'z','x'}, dimensions={0} | all-to-all | bytes 184320 | tf_op jit(solution)/shard_map/all_to_all | solution.py:276
  101.3 0.8 fusion.2
  (29 shorter events, 1.1 us)
Async XLA Ops:
  0.0 8.8 %copy-start = (bf16[16,2880]{1,0:T(8,128)(2,1)S(1)}, bf16[16,2880]{1,0:T(8,128)(2,1)}, u32[]{:S(2)}) copy-start(bf16[16,2880]{1,0:T(8,128)(2,1)} %param.12) | copy-start | bytes 276484
  0.0 8.1 %copy-start.5 = (s32[16,4]{0,1:T(4,128)S(1)}, s32[16,4]{0,1:T(4,128)}, u32[]{:S(2)}) copy-start(s32[16,4]{0,1:T(4,128)} %param.21) | copy-start | bytes 772
  0.0 8.1 %copy-start.4 = (s32[16,4]{0,1:T(4,128)S(1)}, s32[16,4]{0,1:T(4,128)}, u32[]{:S(2)}) copy-start(s32[16,4]{0,1:T(4,128)} %param.20) | copy-start | bytes 772
  0.0 33.7 %copy-start.2 = (bf16[1,2880,360]{1,2,0:T(8,128)(2,1)S(1)}, bf16[1,2880,360]{1,2,0:T(8,128)(2,1)}, u32[]{:S(2)}) copy-start(bf16[1,2880,360]{1,2,0:T(8,128)(2,1)} %param.22) | copy-start | bytes 6220804
  0.0 33.7 %copy-start.3 = (f32[2880]{0:T(1024)S(1)}, f32[2880]{0:T(1024)}, u32[]{:S(2)}) copy-start(f32[2880]{0:T(1024)} %param.19) | copy-start | bytes 34564
  3.6 10.3 %all-to-all-start = ((bf16[8,16,360]{2,1,0:T(8,128)(2,1)}), bf16[8,16,360]{2,1,0:T(8,128)(2,1)S(1)}, u32[]{:S(2)}, u32[]{:S(2)}) async-start(bf16[8,16,360]{2,1,0:T(8,128)(2,1)} %attend.1), calls=%async_computation | async-start | bytes 196608 | tf_op jit(solution)/shard_map/all_to_all | solution.py:209
  15.0 33.8 %all-to-all-start.1 = ((bf16[64,2,360]{2,1,0:T(2,128)(2,1)}), bf16[64,2,360]{2,1,0:T(2,128)(2,1)S(1)}, u32[]{:S(2)}, u32[]{:S(2)}) async-start(bf16[64,2,360]{2,1,0:T(2,128)(2,1)} %reshape.51), calls=%async_computation.1 | async-start | bytes 196608 | tf_op jit(solution)/shard_map/all_to_all | solution.py:239
  58.8 3.6 %collective-permute-start = (bf16[4,360,128]{2,1,0:T(8,128)(2,1)S(1)}, bf16[4,360,128]{2,1,0:T(8,128)(2,1)S(1)}, u32[]{:S(2)}, u32[]{:S(2)}) collective-permute-start(bf16[4,360,128]{2,1,0:T(8,128)(2,1)S(1)} %all_to_all.25), channel_id=1, source_target_pairs={{0,1},{1,0},{2,3},{3,2},{4,5},{5,4},{6,7},{7,6},{8,9},{9,8},{10,11... | collective-permute-start | bytes 1105928 | tf_op jit(solution)/shard_map/ppermute | solution.py:246
  60.7 1.8 %copy-start.1 = (bf16[360,2880]{1,0:T(8,128)(2,1)S(1)}, bf16[360,2880]{1,0:T(8,128)(2,1)}, u32[]{:S(2)}) copy-start(bf16[360,2880]{1,0:T(8,128)(2,1)} %fusion.1.w_ref) | copy-start | bytes 6220804
  64.0 3.6 %collective-permute-start.1 = (bf16[1440,128]{1,0:T(8,128)(2,1)S(1)}, bf16[1440,128]{1,0:T(8,128)(2,1)S(1)}, u32[]{:S(2)}, u32[]{:S(2)}) collective-permute-start(bf16[1440,128]{1,0:T(8,128)(2,1)S(1)} %get-tuple-element.18), channel_id=1, source_target_pairs={{0,1},{1,0},{2,3},{3,2},{4,5},{5,4},{6,7},{7,6},{8,9},{9,8},{10,11... | collective-permute-start | bytes 1105928 | tf_op jit(solution)/shard_map/ppermute | solution.py:264

commit v2 on v1

--- a/solution.py
+++ b/solution.py
@@ -1,5 +1,3 @@
-import functools
-
 import jax
 import jax.numpy as jnp
 from jax import lax
@@ -24,13 +22,22 @@
     kv_hbm,
     new_hbm,
     proj_hbm,
+    ids_hbm,
+    scale_hbm,
+    resid_hbm,
     out_ref,
+    pick_ref,
+    combine_ref,
+    share_ref,
     pos_ref,
     sink_ref,
     q_ref,
     kv_ref,
     new_ref,
     proj_ref,
+    ids_ref,
+    scale_ref,
+    resid_ref,
     sems,
 ):
     rows, window, width = kv_ref.shape
@@ -38,21 +45,57 @@
     copies = [
         pltpu.make_async_copy(src, dst, sems.at[i])
         for i, (src, dst) in enumerate(
-            [(q_hbm, q_ref), (new_hbm, new_ref), (pos_hbm, pos_ref), (sink_hbm, sink_ref)]
+            [
+                (q_hbm, q_ref),
+                (new_hbm, new_ref),
+                (pos_hbm, pos_ref),
+                (sink_hbm, sink_ref),
+                (ids_hbm, ids_ref),
+                (scale_hbm, scale_ref),
+                (resid_hbm, resid_ref),
+            ]
         )
     ]
+    first = len(copies)
     kv_copies = [
         pltpu.make_async_copy(
-            kv_hbm.at[pl.ds(i * piece, piece)], kv_ref.at[pl.ds(i * piece, piece)], sems.at[4 + i]
+            kv_hbm.at[pl.ds(i * piece, piece)], kv_ref.at[pl.ds(i * piece, piece)], sems.at[first + i]
         )
         for i in range(KV_PIECES)
     ]
-    proj_copy = pltpu.make_async_copy(proj_hbm, proj_ref, sems.at[4 + KV_PIECES])
+    proj_copy = pltpu.make_async_copy(proj_hbm, proj_ref, sems.at[first + KV_PIECES])
     for copy in copies + kv_copies:
         copy.start()
     proj_copy.start()
     for copy in copies:
         copy.wait()
+
+    line = lax.broadcasted_iota(jnp.int32, pick_ref.shape, 0)
+    named = jnp.zeros(pick_ref.shape, jnp.float32)
+    weighted = jnp.zeros(pick_ref.shape, jnp.float32)
+    for k in range(ids_ref.shape[0]):
+        match = ids_ref[k : k + 1, :] == line // 2
+        named = jnp.where(match, 1.0, named)
+        weighted = jnp.where(
+            match, scale_ref[k : k + 1, :].astype(jnp.float32) / 65536.0, weighted
+        )
+    ahead = lax.broadcasted_iota(jnp.int32, (rows, rows), 0) < lax.broadcasted_iota(
+        jnp.int32, (rows, rows), 1
+    )
+    before = jnp.dot(
+        named, ahead.astype(jnp.float32), preferred_element_type=jnp.float32
+    ).astype(jnp.int32)
+    kept = before == line % 2
+    pick_ref[...] = jnp.where(kept, named, 0.0).astype(jnp.bfloat16)
+    combine_ref[...] = jnp.where(kept, weighted, 0.0)
+    width_here = share_ref.shape[1]
+    here = lax.axis_index("y") * 2 + lax.axis_index("core")
+    for s in range(out_ref.shape[0]):
+
+        @pl.when(here == s)
+        def _(s=s):
+            share_ref[...] = resid_ref[:, s * width_here : (s + 1) * width_here]
+
     half = width // 2
     groups = 4
     shares, _, share_width = out_ref.shape
@@ -120,15 +163,23 @@
         ).astype(jnp.bfloat16)
 
 
-def attend(positions, sink_logits, queries, kv_cache, new_kv, out_proj):
+def attend(
+    positions, sink_logits, queries, kv_cache, new_kv, out_proj, route_ids, route_weights, residual
+):
     rows, _, window, width = kv_cache.shape
+    slots = 2 * lax.axis_size(GRP)
     features = out_proj.shape[2]
     hbm = pl.BlockSpec(memory_space=pltpu.HBM)
     return pl.pallas_call(
         attend_kernel,
-        out_shape=jax.ShapeDtypeStruct((8, rows, features // 8), jnp.bfloat16),
-        in_specs=[hbm] * 6,
-        out_specs=pl.BlockSpec(memory_space=pltpu.VMEM),
+        out_shape=(
+            jax.ShapeDtypeStruct((8, rows, features // 8), jnp.bfloat16),
+            jax.ShapeDtypeStruct((slots, rows), jnp.bfloat16),
+            jax.ShapeDtypeStruct((slots, rows), jnp.float32),
+            jax.ShapeDtypeStruct((rows, features // 8), jnp.bfloat16),
+        ),
+        in_specs=[hbm] * 9,
+        out_specs=(pl.BlockSpec(memory_space=pltpu.VMEM),) * 4,
         scratch_shapes=[
             pltpu.SMEM((rows,), jnp.int32),
             pltpu.SMEM(sink_logits.shape, jnp.float32),
@@ -136,7 +187,10 @@
             pltpu.VMEM((rows, window, width), jnp.bfloat16),
             pltpu.VMEM((rows, width), jnp.bfloat16),
             pltpu.VMEM((features, out_proj.shape[1]), jnp.bfloat16),
-            pltpu.SemaphoreType.DMA((5 + KV_PIECES,)),
+            pltpu.VMEM(route_ids.shape[::-1], jnp.int32),
+            pltpu.VMEM(route_weights.shape[::-1], jnp.int32),
+            pltpu.VMEM(residual.shape, jnp.bfloat16),
+            pltpu.SemaphoreType.DMA((8 + KV_PIECES,)),
         ],
         compiler_params=pltpu.CompilerParams(vmem_limit_bytes=8 * MIB),
         name="attend",
@@ -150,32 +204,42 @@
                 kv_cache.reshape(rows, window, width),
                 new_kv.reshape(rows, width),
                 jnp.swapaxes(out_proj[0], 0, 1),
+                route_ids.T,
+                route_weights.T,
+                residual,
             )
         )
     )
 
 
-def up_kernel(core_ref, x_ref, w_ref, down_ref, act_ref, send_ref, held_ref):
-    other = 1 - core_ref[0]
+def fold_kernel(w_ref, gain_ref, out_ref):
+    out_ref[...] = (w_ref[...].astype(jnp.float32) * gain_ref[...]).astype(jnp.bfloat16)
+
+
+def expert_kernel(x_ref, w_ref, down_ref, send_ref, own_ref, held_ref):
     x = x_ref[...]
     wide = x.astype(jnp.float32)
     mean_square = jnp.mean(wide * wide, axis=0, keepdims=True)
     projected = jnp.dot(w_ref[...], x, preferred_element_type=jnp.float32)
     held_ref[...] = projected * lax.rsqrt(mean_square + epsilon)
-    hidden_units = held_ref.shape[0] // 2
-    gate = held_ref[pl.ds(0, hidden_units, stride=2), :]
-    up = held_ref[pl.ds(1, hidden_units, stride=2), :]
+    units = held_ref.shape[0] // 2
+    gate = held_ref[pl.ds(0, units, stride=2), :]
+    up = held_ref[pl.ds(1, units, stride=2), :]
     act = ((up + 1.0) * gate * jax.nn.sigmoid(swish_alpha * gate)).astype(jnp.bfloat16)
-    act_ref[...] = act
-    send_ref[...] = jnp.dot(
-        down_ref[other], act, preferred_element_type=jnp.float32
-    ).astype(jnp.bfloat16)
-
-
-def down_kernel(core_ref, act_ref, down_ref, out_ref):
-    out_ref[...] = jnp.dot(
-        down_ref[core_ref[0]], act_ref[...], preferred_element_type=jnp.float32
-    )
+    partial = lax.dot_general(
+        act, down_ref[...], (((0,), (0,)), ((), ())), preferred_element_type=jnp.float32
+    )
+    y_size = send_ref.shape[0]
+    share = down_ref.shape[1] // (2 * y_size)
+    for c in range(2):
+
+        @pl.when(lax.axis_index("core") == c)
+        def _(c=c):
+            for y in range(y_size):
+                start = (2 * y + 1 - c) * share
+                send_ref[y, :, :share] = partial[:, start : start + share].astype(jnp.bfloat16)
+                start = (2 * y + c) * share
+                own_ref[y, :, :share] = partial[:, start : start + share]
 
 
 def local(
@@ -197,88 +261,74 @@
     shares = lax.axis_size(HEAD)
     y_size = lax.axis_size("y")
     share = features // shares
-    topk = route_ids.shape[1]
     capacity = 2
     slots = experts * capacity
     units = w_down.shape[1]
-    core = lax.axis_index("core").astype(jnp.int32).reshape(1)
     vmem = pl.BlockSpec(memory_space=pltpu.VMEM)
-    smem = pl.BlockSpec(memory_space=pltpu.SMEM)
-
-    parts = attend(positions, sink_logits, queries, kv_cache, new_kv, out_proj)
+
+    parts, pick, combine, resid_here = attend(
+        positions,
+        sink_logits,
+        queries,
+        kv_cache,
+        new_kv,
+        out_proj,
+        route_ids,
+        route_weights,
+        residual,
+    )
     parts = lax.all_to_all(parts, HEAD, 0, 0, tiled=True)
     attention = jnp.sum(parts.astype(jnp.float32), axis=0)
-    resid_here = lax.optimization_barrier(
-        lax.dynamic_slice_in_dim(residual, lax.axis_index(HEAD) * share, share, 1)
-    )
     hidden = (resid_here.astype(jnp.float32) + attention).astype(jnp.bfloat16)
 
-    flat_ids = route_ids.reshape(-1)
-    order = jnp.arange(rows * topk, dtype=jnp.int32)
-    earlier = (flat_ids[:, None] == flat_ids[None, :]) & (order[:, None] > order[None, :])
-    slot = (flat_ids * capacity + jnp.sum(earlier.astype(jnp.int32), axis=1)).reshape(rows, topk)
-    hit = slot[:, :, None] == jnp.arange(slots, dtype=jnp.int32)[None, None, :]
-    scale = route_weights.astype(jnp.float32) / 65536.0
-    pick, combine = lax.optimization_barrier(
-        (
-            jnp.sum(hit.astype(jnp.float32), axis=1).astype(jnp.bfloat16),
-            jnp.sum(jnp.where(hit, scale[:, :, None], 0.0), axis=1),
-        )
-    )
-
-    gate_up = (
-        jnp.swapaxes(w_gate_up[0], 0, 1).astype(jnp.float32) * norm_gain[None, :]
-    ).astype(jnp.bfloat16)
-    down = (
-        w_down[0].reshape(units, y_size, 2, share).transpose(2, 1, 3, 0).reshape(2, -1, units)
-    )
-
-    outgoing = lax.dot_general(
-        pick, hidden, (((0,), (0,)), ((), ())), preferred_element_type=jnp.float32
-    ).astype(jnp.bfloat16)
+    outgoing = jnp.dot(pick, hidden, preferred_element_type=jnp.float32).astype(jnp.bfloat16)
     got = lax.all_to_all(outgoing.reshape(experts, capacity, share), GRP, 0, 0, tiled=True)
-    got, gate_up, down = lax.optimization_barrier((got, gate_up, down))
     got = jnp.swapaxes(got.reshape(slots, share), 0, 1)
     mine = lax.all_to_all(
         jnp.broadcast_to(got[None], (y_size, share, slots)), "y", 0, 0, tiled=True
     )
+    gate_up, gain, mine = lax.optimization_barrier(
+        (jnp.swapaxes(w_gate_up[0], 0, 1), norm_gain, mine)
+    )
+    gate_up = pl.pallas_call(
+        fold_kernel,
+        out_shape=jax.ShapeDtypeStruct(gate_up.shape, jnp.bfloat16),
+        in_specs=[vmem, vmem],
+        out_specs=vmem,
+        compiler_params=pltpu.CompilerParams(vmem_limit_bytes=16 * MIB),
+        name="fold",
+    )(gate_up, gain.reshape(1, -1))
     swap = [(0, 1), (1, 0)]
     theirs = lax.ppermute(mine, "core", swap)
-    is_low = core[0] == 0
+    is_low = lax.axis_index("core") == 0
     full = jnp.stack(
         [jnp.where(is_low, mine, theirs), jnp.where(is_low, theirs, mine)], axis=1
     ).reshape(features, slots)
 
-    act, sent = pl.pallas_call(
-        up_kernel,
+    lanes = pl.cdiv(share, 128) * 128
+    sent, own = pl.pallas_call(
+        expert_kernel,
         out_shape=(
-            jax.ShapeDtypeStruct((units, slots), jnp.bfloat16),
-            jax.ShapeDtypeStruct((y_size * share, slots), jnp.bfloat16),
+            jax.ShapeDtypeStruct((y_size, slots, lanes), jnp.bfloat16),
+            jax.ShapeDtypeStruct((y_size, slots, lanes), jnp.float32),
         ),
-        in_specs=[smem, vmem, vmem, vmem],
+        in_specs=[vmem, vmem, vmem],
         out_specs=(vmem, vmem),
         scratch_shapes=[pltpu.VMEM((2 * units, slots), jnp.float32)],
-        compiler_params=pltpu.CompilerParams(vmem_limit_bytes=12 * MIB),
-        name="up",
-    )(core, full, gate_up, down)
+        compiler_params=pltpu.CompilerParams(vmem_limit_bytes=16 * MIB),
+        name="expert",
+    )(full, gate_up, w_down[0])
     arrived = lax.ppermute(sent, "core", swap)
-    own = pl.pallas_call(
-        down_kernel,
-        out_shape=jax.ShapeDtypeStruct((y_size * share, slots), jnp.float32),
-        in_specs=[smem, vmem, vmem],
-        out_specs=vmem,
-        compiler_params=pltpu.CompilerParams(vmem_limit_bytes=12 * MIB),
-        name="down",
-    )(core, act, down)
     paired = (own + arrived.astype(jnp.float32)).astype(jnp.bfloat16)
-    paired = lax.all_to_all(paired.reshape(y_size, share, slots), "y", 0, 0, tiled=True)
-    summed = jnp.sum(paired.astype(jnp.float32), axis=0).astype(jnp.bfloat16)
+    paired = lax.all_to_all(paired, "y", 0, 0, tiled=True)
+    summed = jnp.sum(paired[:, :, :share].astype(jnp.float32), axis=0).astype(jnp.bfloat16)
     back = lax.all_to_all(
-        jnp.swapaxes(summed, 0, 1).reshape(experts, capacity, share), GRP, 0, 0, tiled=True
-    )
-    mixture = jnp.dot(
+        summed.reshape(experts, capacity, share), GRP, 0, 0, tiled=True
+    )
+    mixture = lax.dot_general(
         combine,
         back.reshape(slots, share).astype(jnp.float32),
+        (((0,), (0,)), ((), ())),
         precision=lax.Precision.HIGHEST,
     )
     return (hidden.astype(jnp.float32) + mixture).astype(jnp.bfloat16)

time: 102 us -> 99.7 us (0.977)
  blocking collectives: 42.9 us -> 84.8 us
  starting transfers between devices: 27.2 us -> 4.17 us
  waiting for transfers between devices: 15.3 us -> 2.59 us
  local copies, waits for them, and re-layouts: 7.62 us -> 0.61 us
  other arithmetic: 2.28 us -> 0.3 us
    all_to_all x2 -> x4, blocking collectives: 33.3 us -> 75.2 us  [the longest x1 33.6 us: local(): lax.all_to_all(outgoing.reshape(experts, capacity, share), GRP, 0, 0, til...]
    all_to_all x2 -> x0, starting transfers between devices: 23.1 us -> none  [the longest x1 18.6 us: local(): lax.all_to_all(outgoing.reshape(experts, capacity, share), GRP, 0, 0, til...]
    all_to_all x2 -> x0, waiting for transfers between devices: 12.7 us -> none  [the longest x1 7.63 us: local(): lax.all_to_all(outgoing.reshape(experts, capacity, share), GRP, 0, 0, til...]
    another operation x2 -> x0, local copies, waits for them, and re-layouts: 5.81 us -> none  [local(): w_down[0].reshape(units, y_size, 2, share).transpose(2, 1, 3, 0)]
    convert_element_type x1 -> x0, other arithmetic: 1.71 us -> none  [local(): gate_up = (jnp.swapaxes(w_gate_up[0], 0, 1).astype(jnp.float32) * norm_ga...]
  transfers between devices with their start and end apart: 4 -> 2, of which waited for: 4 -> 2; matrix products, arithmetic and copies ran while one was open for 8% -> 0% of each run, Pallas kernels for 0% -> 0%
where the time goes in v2:
time: 99.7 us; the launch traced here: 99.3 us
  blocking collectives  84.8 us (85%)
  Pallas kernels  5.59 us (6%)
  starting transfers between devices  4.17 us (4%)
  waiting for transfers between devices  2.59 us (3%)
  matrix products  1.08 us (1%)
    all_to_all x1, blocking collectives, local(): lax.all_to_all(outgoing.reshape(experts, capacity, share), GRP, 0, 0, til...  33.6 us
    all_to_all x1, blocking collectives, local(): lax.all_to_all(summed.reshape(experts, capacity, share), GRP, 0, 0, tiled...  20.2 us
    all_to_all x1, blocking collectives, local(): paired = lax.all_to_all(paired, 'y', 0, 0, tiled=True)  11.3 us
    all_to_all x1, blocking collectives, local(): parts = lax.all_to_all(parts, HEAD, 0, 0, tiled=True)  10.1 us
    all_to_all x1, blocking collectives, local(): lax.all_to_all(jnp.broadcast_to(got[None], (y_size, share, slots)), 'y',...  9.63 us
    pallas_call x1, Pallas kernels, attend(): pl.pallas_call(attend_kernel, out_shape=(jax.ShapeDtypeStruct((8, rows, f...  3.27 us
    ppermute x1, starting transfers between devices, local(): arrived = lax.ppermute(sent, 'core', swap)  2.26 us
  transfers between devices with their start and end apart: 2, of which 2 were waited for; matrix products, arithmetic and copies ran while one was open for 0% of the time, Pallas kernels for 0%

profile of v2, /device:TPU:2, one launch (start us, length us, event | category | flops | bytes accessed | tf_op | source)
XLA Modules:
  0.0 99.3 jit_solution(17634876105480929697)
XLA Ops:
  0.0 3.3 %attend.1 = (bf16[8,16,360]{2,1,0:T(8,128)(2,1)S(1)}, bf16[128,16]{1,0:T(8,128)(2,1)S(1)}, f32[128,16]{1,0:T(8,128)S(1)}, bf16[16,360]{1,0:T(8,128)(2,1)S(1)}) custom-call(s32[16]{0:T(128)} %pos_hbm.1, f32[1,4]{1,0:T(1,128)} %sink_hbm.1, bf16[16,256]{1,0:T(8,128)(2,1)} %bitcast.29, bf16[16,128,128]{2,1,0:T(8,128)(2,1)} %bitcast.27, ...), custom_call_target="tpu_custom_call" | custom-call | tf_op jit(solution)/shard_map/attend/pallas_call | solution.py:173
  3.3 10.1 %all_to_all.25 = bf16[8,16,360]{2,1,0:T(8,128)(2,1)S(1)} all-to-all(bf16[8,16,360]{2,1,0:T(8,128)(2,1)S(1)} %get-tuple-element.15), channel_id=1, replica_groups=mesh['z'=16,'x'=4,'y'=4,'core'=2] {'y','core'}, dimensions={0} | all-to-all | bytes 184320 | tf_op jit(solution)/shard_map/all_to_all | solution.py:280
  13.4 0.2 convolution_convert_fusion
  13.7 0.1 copy.14
  13.8 0.1 reshape.31
  13.9 33.6 %all_to_all.26 = bf16[64,2,360]{2,1,0:T(2,128)(2,1)S(1)} all-to-all(bf16[64,2,360]{2,1,0:T(2,128)(2,1)S(1)} %reshape.31), channel_id=1, replica_groups=mesh['z'=16,'x'=4,'y'=4,'core'=2] {'z','x'}, dimensions={0} | all-to-all | bytes 184320 | tf_op jit(solution)/shard_map/all_to_all | solution.py:285
  47.5 0.1 reshape.32
  47.6 0.1 copy.15
  47.8 9.6 %all_to_all.27 = bf16[4,360,128]{2,1,0:T(8,128)(2,1)S(1)} all-to-all(bf16[4,360,128]{2,1,0:T(8,128)(2,1)S(1)} %broadcast_in_dim.2), channel_id=1, replica_groups=mesh['z'=16,'x'=4,'y'=4,'core'=2] {'y'}, dimensions={0} | all-to-all | bytes 737280 | tf_op jit(solution)/shard_map/all_to_all | solution.py:287
  57.4 1.9 %collective-permute-start = (bf16[4,360,128]{2,1,0:T(8,128)(2,1)S(1)}, bf16[4,360,128]{2,1,0:T(8,128)(2,1)S(1)}, u32[]{:S(2)}, u32[]{:S(2)}) collective-permute-start(bf16[4,360,128]{2,1,0:T(8,128)(2,1)S(1)} %all_to_all.27), channel_id=1, source_target_pairs={{0,1},{1,0},{2,3},{3,2},{4,5},{5,4},{6,7},{7,6},{8,9},{9,8},{10,11... | collective-permute-start | bytes 1105928 | tf_op jit(solution)/shard_map/ppermute | solution.py:302
  59.4 0.3 fold.1.w_ref
  59.7 1.2 %collective-permute-done = bf16[4,360,128]{2,1,0:T(8,128)(2,1)S(1)} collective-permute-done((bf16[4,360,128]{2,1,0:T(8,128)(2,1)S(1)}, bf16[4,360,128]{2,1,0:T(8,128)(2,1)S(1)}, u32[]{:S(2)}, u32[]{:S(2)}) %collective-permute-start) | collective-permute-done | bytes 368672 | tf_op jit(solution)/shard_map/ppermute | solution.py:302
  61.0 0.1 select_bitcast_fusion.1
  61.0 0.1 pad_maximum_fusion
  61.1 2.0 %expert.1 = (bf16[4,128,384]{2,1,0:T(8,128)(2,1)S(1)}, f32[4,128,384]{2,1,0:T(8,128)S(1)}) custom-call(bf16[2880,128]{1,0:T(8,128)(2,1)S(1)} %bitcast.23, bf16[360,2880]{1,0:T(8,128)(2,1)S(1)} %fold.1.w_ref, bf16[180,2880]{1,0:T(8,128)(2,1)S(1)} %bitcast.25), custom_call_target="tpu_custom_call" | custom-call | tf_op jit(solution)/shard_map/expert/pallas_call | solution.py:309
  63.1 2.3 %collective-permute-start.1 = (bf16[4,128,384]{2,1,0:T(8,128)(2,1)S(1)}, bf16[4,128,384]{2,1,0:T(8,128)(2,1)S(1)}, u32[]{:S(2)}, u32[]{:S(2)}) collective-permute-start(bf16[4,128,384]{2,1,0:T(8,128)(2,1)S(1)} %get-tuple-element.22), channel_id=1, source_target_pairs={{0,1},{1,0},{2,3},{3,2},{4,5},{5,4},{6,7},{7,6},{8,9},{9,8},{10,11... | collective-permute-start | bytes 1179656 | tf_op jit(solution)/shard_map/ppermute | solution.py:321
  65.4 1.3 %collective-permute-done.1 = bf16[4,128,384]{2,1,0:T(8,128)(2,1)S(1)} collective-permute-done((bf16[4,128,384]{2,1,0:T(8,128)(2,1)S(1)}, bf16[4,128,384]{2,1,0:T(8,128)(2,1)S(1)}, u32[]{:S(2)}, u32[]{:S(2)}) %collective-permute-start.1) | collective-permute-done | bytes 393248 | tf_op jit(solution)/shard_map/ppermute | solution.py:321
  66.7 0.1 add_convert_fusion
  66.8 11.3 %all_to_all.28 = bf16[4,128,384]{2,1,0:T(8,128)(2,1)S(1)} all-to-all(bf16[4,128,384]{2,1,0:T(8,128)(2,1)S(1)} %add_convert_fusion), channel_id=1, replica_groups=mesh['z'=16,'x'=4,'y'=4,'core'=2] {'y'}, dimensions={0} | all-to-all | bytes 786432 | tf_op jit(solution)/shard_map/all_to_all | solution.py:323
  78.1 0.1 slice_reduce_fusion
  78.2 0.1 reshape.35
  78.2 20.2 %all_to_all.29 = bf16[64,2,360]{2,1,0:T(2,128)(2,1)S(1)} all-to-all(bf16[64,2,360]{2,1,0:T(2,128)(2,1)S(1)} %reshape.35), channel_id=1, replica_groups=mesh['z'=16,'x'=4,'y'=4,'core'=2] {'z','x'}, dimensions={0} | all-to-all | bytes 184320 | tf_op jit(solution)/shard_map/all_to_all | solution.py:325
  98.4 0.1 reshape.36
  98.5 0.8 fusion
  (9 shorter events, 0.1 us)
Async XLA Ops:
  0.0 59.3 %copy-start.2 = (f32[2880]{0:T(1024)S(1)}, f32[2880]{0:T(1024)}, u32[]{:S(2)}) copy-start(f32[2880]{0:T(1024)} %param.19) | copy-start | bytes 34564
  0.0 59.4 %copy-start = (bf16[1,2880,360]{1,2,0:T(8,128)(2,1)S(1)}, bf16[1,2880,360]{1,2,0:T(8,128)(2,1)}, u32[]{:S(2)}) copy-start(bf16[1,2880,360]{1,2,0:T(8,128)(2,1)} %param.22) | copy-start | bytes 6220804
  57.4 3.6 %collective-permute-start = (bf16[4,360,128]{2,1,0:T(8,128)(2,1)S(1)}, bf16[4,360,128]{2,1,0:T(8,128)(2,1)S(1)}, u32[]{:S(2)}, u32[]{:S(2)}) collective-permute-start(bf16[4,360,128]{2,1,0:T(8,128)(2,1)S(1)} %all_to_all.27), channel_id=1, source_target_pairs={{0,1},{1,0},{2,3},{3,2},{4,5},{5,4},{6,7},{7,6},{8,9},{9,8},{10,11... | collective-permute-start | bytes 1105928 | tf_op jit(solution)/shard_map/ppermute | solution.py:302
  59.7 1.4 %copy-start.1 = (bf16[1,180,2880]{2,1,0:T(8,128)(2,1)S(1)}, bf16[1,180,2880]{2,1,0:T(8,128)(2,1)}, u32[]{:S(2)}) copy-start(bf16[1,180,2880]{2,1,0:T(8,128)(2,1)} %param.23) | copy-start | bytes 3110404
  63.1 3.6 %collective-permute-start.1 = (bf16[4,128,384]{2,1,0:T(8,128)(2,1)S(1)}, bf16[4,128,384]{2,1,0:T(8,128)(2,1)S(1)}, u32[]{:S(2)}, u32[]{:S(2)}) collective-permute-start(bf16[4,128,384]{2,1,0:T(8,128)(2,1)S(1)} %get-tuple-element.22), channel_id=1, source_target_pairs={{0,1},{1,0},{2,3},{3,2},{4,5},{5,4},{6,7},{7,6},{8,9},{9,8},{10,11... | collective-permute-start | bytes 1179656 | tf_op jit(solution)/shard_map/ppermute | solution.py:321

commit v3 on v2

--- a/solution.py
+++ b/solution.py
@@ -11,8 +11,10 @@
 GRID = (16, 4, 4, 2)
 GRP = ("z", "x")
 HEAD = ("y", "core")
+FEATURES = 2880
 MIB = 1 << 20
 KV_PIECES = 4
+PROJ_PIECES = 4
 
 
 def attend_kernel(
@@ -63,10 +65,18 @@
         )
         for i in range(KV_PIECES)
     ]
-    proj_copy = pltpu.make_async_copy(proj_hbm, proj_ref, sems.at[first + KV_PIECES])
-    for copy in copies + kv_copies:
+    shares = out_ref.shape[0]
+    part = proj_ref.shape[0] // PROJ_PIECES
+    proj_copies = [
+        pltpu.make_async_copy(
+            proj_hbm.at[pl.ds(i * part, part)],
+            proj_ref.at[pl.ds(i * part, part)],
+            sems.at[first + KV_PIECES + i],
+        )
+        for i in range(PROJ_PIECES)
+    ]
+    for copy in copies + kv_copies + proj_copies:
         copy.start()
-    proj_copy.start()
     for copy in copies:
         copy.wait()
 
@@ -98,7 +108,7 @@
 
     half = width // 2
     groups = 4
-    shares, _, share_width = out_ref.shape
+    share_width = out_ref.shape[2]
     lane = lax.broadcasted_iota(jnp.int32, (rows, width), 1)
     row = lax.broadcasted_iota(jnp.int32, (rows, width), 0)
     low = lane < half
@@ -153,8 +163,9 @@
         second = mixed[(2 * pair + 1) * rows : (2 * pair + 2) * rows]
         merged.append(jnp.where(low, pltpu.roll(first, half, 1), second))
     merged = jnp.concatenate(merged, axis=1).astype(jnp.bfloat16)
-    proj_copy.wait()
     for s in range(shares):
+        if s % (shares // PROJ_PIECES) == 0:
+            proj_copies[s // (shares // PROJ_PIECES)].wait()
         out_ref[s] = lax.dot_general(
             merged,
             proj_ref[pl.ds(s * share_width, share_width), :],
@@ -173,10 +184,10 @@
     return pl.pallas_call(
         attend_kernel,
         out_shape=(
-            jax.ShapeDtypeStruct((8, rows, features // 8), jnp.bfloat16),
-            jax.ShapeDtypeStruct((slots, rows), jnp.bfloat16),
-            jax.ShapeDtypeStruct((slots, rows), jnp.float32),
-            jax.ShapeDtypeStruct((rows, features // 8), jnp.bfloat16),
+            pltpu.VMEM((8, rows, features // 8), jnp.bfloat16),
+            pltpu.VMEM((slots, rows), jnp.bfloat16),
+            pltpu.VMEM((slots, rows), jnp.float32),
+            pltpu.VMEM((rows, features // 8), jnp.bfloat16),
         ),
         in_specs=[hbm] * 9,
         out_specs=(pl.BlockSpec(memory_space=pltpu.VMEM),) * 4,
@@ -190,9 +201,9 @@
             pltpu.VMEM(route_ids.shape[::-1], jnp.int32),
             pltpu.VMEM(route_weights.shape[::-1], jnp.int32),
             pltpu.VMEM(residual.shape, jnp.bfloat16),
-            pltpu.SemaphoreType.DMA((8 + KV_PIECES,)),
+            pltpu.SemaphoreType.DMA((7 + KV_PIECES + PROJ_PIECES,)),
         ],
-        compiler_params=pltpu.CompilerParams(vmem_limit_bytes=8 * MIB),
+        compiler_params=pltpu.CompilerParams(vmem_limit_bytes=int(61.4 * MIB)),
         name="attend",
     )(
         *(
@@ -212,34 +223,122 @@
     )
 
 
-def fold_kernel(w_ref, gain_ref, out_ref):
-    out_ref[...] = (w_ref[...].astype(jnp.float32) * gain_ref[...]).astype(jnp.bfloat16)
-
-
-def expert_kernel(x_ref, w_ref, down_ref, send_ref, own_ref, held_ref):
-    x = x_ref[...]
-    wide = x.astype(jnp.float32)
-    mean_square = jnp.mean(wide * wide, axis=0, keepdims=True)
-    projected = jnp.dot(w_ref[...], x, preferred_element_type=jnp.float32)
+def dispatch_kernel(parts_ref, share_ref, pick_ref, hidden_ref, out_ref):
+    summed = jnp.sum(parts_ref[...].astype(jnp.float32), axis=0)
+    hidden = (share_ref[...].astype(jnp.float32) + summed).astype(jnp.bfloat16)
+    hidden_ref[...] = hidden
+    out_ref[...] = jnp.dot(
+        pick_ref[...], hidden, preferred_element_type=jnp.float32
+    ).astype(jnp.bfloat16)
+
+
+def swap_rows(rows, outer, inner):
+    count = rows.shape[0]
+    to = lax.broadcasted_iota(jnp.int32, (count, count), 0)
+    at = lax.broadcasted_iota(jnp.int32, (count, count), 1)
+    source = ((to // 2) % outer) * (2 * inner) + (to // (2 * outer)) * 2 + to % 2
+    return jnp.dot(
+        (at == source).astype(jnp.bfloat16), rows, preferred_element_type=jnp.float32
+    ).astype(jnp.bfloat16)
+
+
+def spread_kernel(got_ref, out_ref):
+    z_size, x_size = GRID[0], GRID[1]
+    share = got_ref.shape[1]
+    rows = swap_rows(got_ref[...], z_size, x_size)
+    rest = jnp.zeros((rows.shape[0], out_ref.shape[2] - share), jnp.bfloat16)
+    for y in range(out_ref.shape[0]):
+        out_ref[y, :, :share] = rows
+        out_ref[y, :, share:] = rest
+
+
+def gather_kernel(parts_ref, out_ref):
+    z_size, x_size = GRID[0], GRID[1]
+    share = out_ref.shape[1]
+    summed = jnp.sum(parts_ref[...].astype(jnp.float32), axis=0)[:, :share]
+    out_ref[...] = swap_rows(summed.astype(jnp.bfloat16), x_size, z_size)
+
+
+def relay_kernel(up_ref, gain_ref, down_hbm, up_out, down_out, down_ref, sem):
+    copy = pltpu.make_async_copy(down_hbm, down_ref, sem)
+    copy.start()
+    y_size = GRID[2]
+    share = down_ref.shape[1] // (2 * y_size)
+    lanes = down_out.shape[2] // y_size
+
+    def lay(source, out):
+        rest = jnp.zeros((source.shape[0], lanes - share), jnp.bfloat16)
+        for y in range(y_size):
+            for c in range(2):
+                start = (2 * y + c) * share
+                out[c, :, y * lanes : y * lanes + share] = source[:, start : start + share]
+                out[c, :, y * lanes + share : (y + 1) * lanes] = rest
+
+    lay((up_ref[...].astype(jnp.float32) * gain_ref[...]).astype(jnp.bfloat16), up_out)
+    copy.wait()
+    lay(down_ref[...], down_out)
+
+
+def joined(ref):
+    return jnp.concatenate([ref[y] for y in range(ref.shape[0])], axis=1)
+
+
+def expert_kernel(mine_ref, theirs_ref, up_ref, down_ref, act_ref, send_ref, held_ref):
+    core = lax.axis_index("core")
+    y_size, slots, lanes = mine_ref.shape
+    units = act_ref.shape[0]
+    projected = jnp.zeros(held_ref.shape, jnp.float32)
+    squares = jnp.zeros((slots, 128), jnp.float32)
+    for ref, index in ((mine_ref, core), (theirs_ref, 1 - core)):
+        x = joined(ref)
+        projected = projected + lax.dot_general(
+            up_ref[index], x, (((1,), (1,)), ((), ())), preferred_element_type=jnp.float32
+        )
+        wide = x.astype(jnp.float32)
+        wide = wide * wide
+        for tile in range(wide.shape[1] // 128):
+            squares = squares + wide[:, tile * 128 : (tile + 1) * 128]
+    mean_square = jnp.sum(jnp.transpose(squares), axis=0, keepdims=True) / FEATURES
     held_ref[...] = projected * lax.rsqrt(mean_square + epsilon)
-    units = held_ref.shape[0] // 2
     gate = held_ref[pl.ds(0, units, stride=2), :]
     up = held_ref[pl.ds(1, units, stride=2), :]
     act = ((up + 1.0) * gate * jax.nn.sigmoid(swish_alpha * gate)).astype(jnp.bfloat16)
+    act_ref[...] = act
     partial = lax.dot_general(
-        act, down_ref[...], (((0,), (0,)), ((), ())), preferred_element_type=jnp.float32
-    )
-    y_size = send_ref.shape[0]
-    share = down_ref.shape[1] // (2 * y_size)
-    for c in range(2):
-
-        @pl.when(lax.axis_index("core") == c)
-        def _(c=c):
-            for y in range(y_size):
-                start = (2 * y + 1 - c) * share
-                send_ref[y, :, :share] = partial[:, start : start + share].astype(jnp.bfloat16)
-                start = (2 * y + c) * share
-                own_ref[y, :, :share] = partial[:, start : start + share]
+        act, down_ref[1 - core], (((0,), (0,)), ((), ())), preferred_element_type=jnp.float32
+    ).astype(jnp.bfloat16)
+    for y in range(y_size):
+        send_ref[y] = partial[:, y * lanes : (y + 1) * lanes]
+
+
+def own_kernel(act_ref, down_ref, out_ref):
+    y_size, _, lanes = out_ref.shape
+    partial = lax.dot_general(
+        act_ref[...],
+        down_ref[lax.axis_index("core")],
+        (((0,), (0,)), ((), ())),
+        preferred_element_type=jnp.float32,
+    )
+    for y in range(y_size):
+        out_ref[y] = partial[:, y * lanes : (y + 1) * lanes]
+
+
+def run(kernel, name, outs, scratch=(), from_hbm=()):
+    vmem = pl.BlockSpec(memory_space=pltpu.VMEM)
+    hbm = pl.BlockSpec(memory_space=pltpu.HBM)
+
+    def call(*operands):
+        return pl.pallas_call(
+            kernel,
+            out_shape=tuple(pltpu.VMEM(shape, dtype) for shape, dtype in outs),
+            in_specs=[hbm if i in from_hbm else vmem for i in range(len(operands))],
+            out_specs=(vmem,) * len(outs),
+            scratch_shapes=list(scratch),
+            compiler_params=pltpu.CompilerParams(vmem_limit_bytes=16 * MIB),
+            name=name,
+        )(*operands)
+
+    return call
 
 
 def local(
@@ -257,14 +356,14 @@
     w_down,
 ):
     rows, features = residual.shape
-    experts = lax.axis_size(GRP)
-    shares = lax.axis_size(HEAD)
-    y_size = lax.axis_size("y")
-    share = features // shares
-    capacity = 2
-    slots = experts * capacity
+    z_size, x_size, y_size, _ = GRID
+    share = features // (2 * y_size)
+    lanes = pl.cdiv(share, 128) * 128
+    slots = 2 * z_size * x_size
     units = w_down.shape[1]
-    vmem = pl.BlockSpec(memory_space=pltpu.VMEM)
+    bf16 = jnp.bfloat16
+    plane = ("y", "x")
+    swap = [(0, 1), (1, 0)]
 
     parts, pick, combine, resid_here = attend(
         positions,
@@ -278,60 +377,52 @@
         residual,
     )
     parts = lax.all_to_all(parts, HEAD, 0, 0, tiled=True)
-    attention = jnp.sum(parts.astype(jnp.float32), axis=0)
-    hidden = (resid_here.astype(jnp.float32) + attention).astype(jnp.bfloat16)
-
-    outgoing = jnp.dot(pick, hidden, preferred_element_type=jnp.float32).astype(jnp.bfloat16)
-    got = lax.all_to_all(outgoing.reshape(experts, capacity, share), GRP, 0, 0, tiled=True)
-    got = jnp.swapaxes(got.reshape(slots, share), 0, 1)
+    hidden, outgoing = run(
+        dispatch_kernel, "dispatch", [((rows, share), bf16), ((slots, share), bf16)]
+    )(parts, resid_here, pick)
+
+    got = lax.all_to_all(outgoing.reshape(z_size, 2 * x_size, share), "z", 0, 0, tiled=True)
+    (spread,) = run(spread_kernel, "spread", [((y_size, slots, lanes), bf16)])(
+        got.reshape(slots, share)
+    )
     mine = lax.all_to_all(
-        jnp.broadcast_to(got[None], (y_size, share, slots)), "y", 0, 0, tiled=True
-    )
-    gate_up, gain, mine = lax.optimization_barrier(
-        (jnp.swapaxes(w_gate_up[0], 0, 1), norm_gain, mine)
-    )
-    gate_up = pl.pallas_call(
-        fold_kernel,
-        out_shape=jax.ShapeDtypeStruct(gate_up.shape, jnp.bfloat16),
-        in_specs=[vmem, vmem],
-        out_specs=vmem,
-        compiler_params=pltpu.CompilerParams(vmem_limit_bytes=16 * MIB),
-        name="fold",
-    )(gate_up, gain.reshape(1, -1))
-    swap = [(0, 1), (1, 0)]
+        spread.reshape(y_size * x_size, 2 * z_size, lanes), plane, 0, 0, tiled=True
+    ).reshape(y_size, slots, lanes)
+    gate_up, down, gain, mine = lax.optimization_barrier(
+        (jnp.swapaxes(w_gate_up[0], 0, 1), w_down[0], norm_gain, mine)
+    )
+    gate_up, down = run(
+        relay_kernel,
+        "relay",
+        [((2, 2 * units, y_size * lanes), bf16), ((2, units, y_size * lanes), bf16)],
+        [pltpu.VMEM((units, features), bf16), pltpu.SemaphoreType.DMA],
+        from_hbm=(2,),
+    )(gate_up, gain.reshape(1, -1), pltpu.with_memory_space_constraint(down, pltpu.HBM))
     theirs = lax.ppermute(mine, "core", swap)
-    is_low = lax.axis_index("core") == 0
-    full = jnp.stack(
-        [jnp.where(is_low, mine, theirs), jnp.where(is_low, theirs, mine)], axis=1
-    ).reshape(features, slots)
-
-    lanes = pl.cdiv(share, 128) * 128
-    sent, own = pl.pallas_call(
+    act, sent = run(
         expert_kernel,
-        out_shape=(
-            jax.ShapeDtypeStruct((y_size, slots, lanes), jnp.bfloat16),
-            jax.ShapeDtypeStruct((y_size, slots, lanes), jnp.float32),
-        ),
-        in_specs=[vmem, vmem, vmem],
-        out_specs=(vmem, vmem),
-        scratch_shapes=[pltpu.VMEM((2 * units, slots), jnp.float32)],
-        compiler_params=pltpu.CompilerParams(vmem_limit_bytes=16 * MIB),
-        name="expert",
-    )(full, gate_up, w_down[0])
+        "expert",
+        [((units, slots), bf16), ((y_size, slots, lanes), bf16)],
+        [pltpu.VMEM((2 * units, slots), jnp.float32)],
+    )(mine, theirs, gate_up, down)
+
     arrived = lax.ppermute(sent, "core", swap)
-    paired = (own + arrived.astype(jnp.float32)).astype(jnp.bfloat16)
-    paired = lax.all_to_all(paired, "y", 0, 0, tiled=True)
-    summed = jnp.sum(paired[:, :, :share].astype(jnp.float32), axis=0).astype(jnp.bfloat16)
-    back = lax.all_to_all(
-        summed.reshape(experts, capacity, share), GRP, 0, 0, tiled=True
-    )
+    (own,) = run(own_kernel, "own", [((y_size, slots, lanes), jnp.float32)])(act, down)
+    paired = (own + arrived.astype(jnp.float32)).astype(bf16)
+    paired = lax.all_to_all(
+        paired.reshape(y_size * x_size, 2 * z_size, lanes), plane, 0, 0, tiled=True
+    )
+    (summed,) = run(gather_kernel, "gather", [((slots, share), bf16)])(
+        paired.reshape(y_size, slots, lanes)
+    )
+    back = lax.all_to_all(summed.reshape(z_size, 2 * x_size, share), "z", 0, 0, tiled=True)
     mixture = lax.dot_general(
         combine,
         back.reshape(slots, share).astype(jnp.float32),
         (((0,), (0,)), ((), ())),
         precision=lax.Precision.HIGHEST,
     )
-    return (hidden.astype(jnp.float32) + mixture).astype(jnp.bfloat16)
+    return (hidden.astype(jnp.float32) + mixture).astype(bf16)
 
 
 def solution(mesh):

time: 99.7 us -> 96.3 us (0.966)
  the two profiles are of different devices: /device:TPU:2 before, /device:TPU:32 now
where the time goes in v3:
time: 96.3 us; the launch traced here: 95.9 us
  blocking collectives  82 us (85%)
  Pallas kernels  7.49 us (8%)
  starting transfers between devices  4.32 us (4%)
  waiting for transfers between devices  1.05 us (1%)
    all_to_all x1, blocking collectives, local(): lax.all_to_all(outgoing.reshape(z_size, 2 * x_size, share), 'z', 0, 0, ti...  27.7 us
    all_to_all x1, blocking collectives, local(): lax.all_to_all(summed.reshape(z_size, 2 * x_size, share), 'z', 0, 0, tile...  16.5 us
    all_to_all x1, blocking collectives, local(): lax.all_to_all(spread.reshape(y_size * x_size, 2 * z_size, lanes), plane,...  14.2 us
    all_to_all x1, blocking collectives, local(): lax.all_to_all(paired.reshape(y_size * x_size, 2 * z_size, lanes), plane,...  13.5 us
    all_to_all x1, blocking collectives, local(): parts = lax.all_to_all(parts, HEAD, 0, 0, tiled=True)  10.1 us
    pallas_call x6, Pallas kernels, call(): pl.pallas_call(kernel, out_shape=tuple((pltpu.VMEM(shape, dtype) for shap...  3.84 us
    pallas_call x1, Pallas kernels, attend(): pl.pallas_call(attend_kernel, out_shape=(pltpu.VMEM((8, rows, features //...  3.65 us
    ppermute x1, starting transfers between devices, local(): arrived = lax.ppermute(sent, 'core', swap)  2.41 us
  transfers between devices with their start and end apart: 2, of which 1 were waited for; matrix products, arithmetic and copies ran while one was open for 0% of the time, Pallas kernels for 2%

profile of v3, /device:TPU:32, one launch (start us, length us, event | category | flops | bytes accessed | tf_op | source)
XLA Modules:
  0.0 95.9 jit_solution(12234048505370884190)
XLA Ops:
  0.0 0.0 copy-start.1
  0.0 0.0 copy-start
  0.0 3.6 %attend.1 = (bf16[8,16,360]{2,1,0:T(8,128)(2,1)S(1)}, bf16[128,16]{1,0:T(8,128)(2,1)S(1)}, f32[128,16]{1,0:T(8,128)S(1)}, bf16[16,360]{1,0:T(8,128)(2,1)S(1)}) custom-call(s32[16]{0:T(128)} %pos_hbm.1, f32[1,4]{1,0:T(1,128)} %sink_hbm.1, bf16[16,256]{1,0:T(8,128)(2,1)} %bitcast.35, bf16[16,128,128]{2,1,0:T(8,128)(2,1)} %bitcast.34, ...), custom_call_target="tpu_custom_call" | custom-call | tf_op jit(solution)/shard_map/attend/pallas_call | solution.py:184
  3.7 10.1 %all_to_all.25.parts_ref = bf16[8,16,360]{2,1,0:T(8,128)(2,1)S(1)} all-to-all(bf16[8,16,360]{2,1,0:T(8,128)(2,1)S(1)} %get-tuple-element.19), channel_id=1, replica_groups=mesh['z'=16,'x'=4,'y'=4,'core'=2] {'y','core'}, dimensions={0} | all-to-all | bytes 184320 | tf_op jit(solution)/shard_map/all_to_all | solution.py:379
  13.8 0.2 dispatch.1
  13.9 27.7 %all_to_all.26 = bf16[16,8,360]{2,1,0:T(8,128)(2,1)S(1)} all-to-all(bf16[16,8,360]{2,1,0:T(8,128)(2,1)S(1)} %bitcast.30), channel_id=1, replica_groups=mesh['z'=16,'x'=4,'y'=4,'core'=2] {'z'}, dimensions={0} | all-to-all | bytes 184320 | tf_op jit(solution)/shard_map/all_to_all | solution.py:384
  41.6 0.2 spread.1
  41.8 14.2 %all_to_all.27 = bf16[16,32,384]{2,1,0:T(8,128)(2,1)S(1)} all-to-all(bf16[16,32,384]{2,1,0:T(8,128)(2,1)S(1)} %bitcast.24), channel_id=1, replica_groups=mesh['z'=16,'x'=4,'y'=4,'core'=2] {'y','x'}, dimensions={0} | all-to-all | bytes 786432 | tf_op jit(solution)/shard_map/all_to_all | solution.py:388
  56.0 1.9 %collective-permute-start = (bf16[4,128,384]{2,1,0:T(8,128)(2,1)S(1)}, bf16[4,128,384]{2,1,0:T(8,128)(2,1)S(1)}, u32[]{:S(2)}, u32[]{:S(2)}) collective-permute-start(bf16[4,128,384]{2,1,0:T(8,128)(2,1)S(1)} %bitcast.26), channel_id=1, source_target_pairs={{0,1},{1,0},{2,3},{3,2},{4,5},{5,4},{6,7},{7,6},{8,9},{9,8},{10,11... | collective-permute-start | bytes 1179656 | tf_op jit(solution)/shard_map/ppermute | solution.py:401
  58.0 0.0 copy-done.1
  58.0 0.0 copy-done
  58.0 1.7 %relay.1 = (bf16[2,360,1536]{2,1,0:T(8,128)(2,1)S(1)}, bf16[2,180,1536]{2,1,0:T(8,128)(2,1)S(1)}) custom-call(bf16[360,2880]{1,0:T(8,128)(2,1)S(1)} %bitcast.23, f32[1,2880]{1,0:T(1,128)S(1)} %reshape.43.gain_ref, bf16[180,2880]{1,0:T(8,128)(2,1)} %bitcast.33), custom_call_target="tpu_custom_call" | custom-call | tf_op jit(solution)/shard_map/relay/pallas_call | solution.py:331
  59.7 0.0 collective-permute-done.theirs_ref
  59.8 1.3 %expert.1 = (bf16[180,128]{1,0:T(8,128)(2,1)S(1)}, bf16[4,128,384]{2,1,0:T(8,128)(2,1)S(1)}) custom-call(bf16[4,128,384]{2,1,0:T(8,128)(2,1)S(1)} %bitcast.27, bf16[4,128,384]{2,1,0:T(8,128)(2,1)S(1)} %collective-permute-done.theirs_ref, bf16[2,360,1536]{2,1,0:T(8,128)(2,1)S(1)} %get-tuple-element.29.up_ref, bf16[2,180,1536]{2,1,0:T(8,128)(2,1)S(1)} %get-tuple-element.30.down_ref), custom_call_target="tpu_custom_call" | custom-call | tf_op jit(solution)/shard_map/expert/pallas_call | solution.py:331
  61.1 2.4 %collective-permute-start.1 = (bf16[4,128,384]{2,1,0:T(8,128)(2,1)S(1)}, bf16[4,128,384]{2,1,0:T(8,128)(2,1)S(1)}, u32[]{:S(2)}, u32[]{:S(2)}) collective-permute-start(bf16[4,128,384]{2,1,0:T(8,128)(2,1)S(1)} %get-tuple-element.32), channel_id=1, source_target_pairs={{0,1},{1,0},{2,3},{3,2},{4,5},{5,4},{6,7},{7,6},{8,9},{9,8},{10,11... | collective-permute-start | bytes 1179656 | tf_op jit(solution)/shard_map/ppermute | solution.py:409
  63.5 0.3 own.1
  63.8 1.0 %collective-permute-done.1 = bf16[4,128,384]{2,1,0:T(8,128)(2,1)S(1)} collective-permute-done((bf16[4,128,384]{2,1,0:T(8,128)(2,1)S(1)}, bf16[4,128,384]{2,1,0:T(8,128)(2,1)S(1)}, u32[]{:S(2)}, u32[]{:S(2)}) %collective-permute-start.1) | collective-permute-done | bytes 393248 | tf_op jit(solution)/shard_map/ppermute | solution.py:409
  64.8 0.1 add_convert_fusion
  64.9 13.5 %all_to_all.28 = bf16[16,32,384]{2,1,0:T(8,128)(2,1)S(1)} all-to-all(bf16[16,32,384]{2,1,0:T(8,128)(2,1)S(1)} %bitcast.31), channel_id=1, replica_groups=mesh['z'=16,'x'=4,'y'=4,'core'=2] {'y','x'}, dimensions={0} | all-to-all | bytes 786432 | tf_op jit(solution)/shard_map/all_to_all | solution.py:412
  78.4 0.2 gather.1
  78.6 16.5 %all_to_all.29 = bf16[16,8,360]{2,1,0:T(8,128)(2,1)S(1)} all-to-all(bf16[16,8,360]{2,1,0:T(8,128)(2,1)S(1)} %bitcast.29), channel_id=1, replica_groups=mesh['z'=16,'x'=4,'y'=4,'core'=2] {'z'}, dimensions={0} | all-to-all | bytes 184320 | tf_op jit(solution)/shard_map/all_to_all | solution.py:418
  95.1 0.8 fusion
  (1 shorter events, 0.0 us)
Async XLA Ops:
  0.0 58.0 %copy-start.1 = (f32[2880]{0:T(1024)S(1)}, f32[2880]{0:T(1024)}, u32[]{:S(2)}) copy-start(f32[2880]{0:T(1024)} %param.19) | copy-start | bytes 34564
  0.0 58.0 %copy-start = (bf16[1,2880,360]{1,2,0:T(8,128)(2,1)S(1)}, bf16[1,2880,360]{1,2,0:T(8,128)(2,1)}, u32[]{:S(2)}) copy-start(bf16[1,2880,360]{1,2,0:T(8,128)(2,1)} %param.22) | copy-start | bytes 6220804
  56.0 3.7 %collective-permute-start = (bf16[4,128,384]{2,1,0:T(8,128)(2,1)S(1)}, bf16[4,128,384]{2,1,0:T(8,128)(2,1)S(1)}, u32[]{:S(2)}, u32[]{:S(2)}) collective-permute-start(bf16[4,128,384]{2,1,0:T(8,128)(2,1)S(1)} %bitcast.26), channel_id=1, source_target_pairs={{0,1},{1,0},{2,3},{3,2},{4,5},{5,4},{6,7},{7,6},{8,9},{9,8},{10,11... | collective-permute-start | bytes 1179656 | tf_op jit(solution)/shard_map/ppermute | solution.py:401
  61.1 3.7 %collective-permute-start.1 = (bf16[4,128,384]{2,1,0:T(8,128)(2,1)S(1)}, bf16[4,128,384]{2,1,0:T(8,128)(2,1)S(1)}, u32[]{:S(2)}, u32[]{:S(2)}) collective-permute-start(bf16[4,128,384]{2,1,0:T(8,128)(2,1)S(1)} %get-tuple-element.32), channel_id=1, source_target_pairs={{0,1},{1,0},{2,3},{3,2},{4,5},{5,4},{6,7},{7,6},{8,9},{9,8},{10,11... | collective-permute-start | bytes 1179656 | tf_op jit(solution)/shard_map/ppermute | solution.py:409

commit v4 on v3

v4 whole, which is shorter than its diff:
```python
import jax
import jax.numpy as jnp
from jax import lax
from jax.experimental import pallas as pl
from jax.experimental.pallas import tpu as pltpu
from jax.sharding import Mesh, PartitionSpec as P

epsilon = 1e-05
swish_alpha = 1.702

GRID = (16, 4, 4, 2)
GRP = ("z", "x")
HEAD = ("y", "core")
PLANE = ("y", "x")
FEATURES = 2880
MIB = 1 << 20


def attend_kernel(
    pos_hbm,
    sink_hbm,
    q_hbm,
    kv_hbm,
    new_hbm,
    proj_hbm,
    out_ref,
    pos_ref,
    sink_ref,
    q_ref,
    kv_ref,
    new_ref,
    proj_ref,
    sems,
):
    rows, window, width = kv_ref.shape
    shares = out_ref.shape[0]
    q_copy, kv_copy, new_copy, pos_copy, sink_copy, proj_copy = (
        pltpu.make_async_copy(src, dst, sems.at[i])
        for i, (src, dst) in enumerate(
            [
                (q_hbm, q_ref),
                (kv_hbm, kv_ref),
                (new_hbm, new_ref),
                (pos_hbm, pos_ref),
                (sink_hbm, sink_ref),
                (proj_hbm, proj_ref),
            ]
        )
    )
    for copy in (q_copy, kv_copy, new_copy, pos_copy, sink_copy, proj_copy):
        copy.start()
    half = width // 2
    groups = 4
    share_width = out_ref.shape[2]
    lane = lax.broadcasted_iota(jnp.int32, (rows, width), 1)
    low = lane < half
    q_copy.wait()
    q = q_ref[...].astype(jnp.float32)
    parts = []
    for pair in range(groups // 2):
        both = q[:, pair * width : (pair + 1) * width]
        parts.append(jnp.where(low, both, 0.0))
        parts.append(jnp.where(low, pltpu.roll(both, half, 1), 0.0))
    stacked = jnp.concatenate(parts, axis=0)
    stacked_low = stacked.astype(jnp.bfloat16)
    shape = (groups * rows, window)
    lanes = lax.broadcasted_iota(jnp.int32, shape, 1)
    request = lax.broadcasted_iota(jnp.int32, shape, 0) % rows

    kv_copy.wait()
    kv = kv_ref[...].reshape(rows * window, width)
    found = lax.dot_general(
        stacked_low, kv, (((1,), (1,)), ((), ())), preferred_element_type=jnp.float32
    )
    scores = jnp.zeros(shape, jnp.float32)
    for t in range(rows):
        scores = jnp.where(request == t, found[:, t * window : (t + 1) * window], scores)
    for copy in (new_copy, pos_copy, sink_copy):
        copy.wait()
    new = new_ref[...].astype(jnp.float32)
    new_all = jnp.concatenate([new] * groups, axis=0)
    square = (rows, rows)
    diagonal = lax.broadcasted_iota(jnp.int32, square, 0) == lax.broadcasted_iota(
        jnp.int32, square, 1
    )
    pos = jnp.sum(jnp.where(diagonal, pos_ref[...], 0), axis=1, keepdims=True)
    pos = jnp.concatenate([jnp.broadcast_to(pos, (rows, width))] * groups, axis=0)
    heads = (groups * rows, groups)
    of_head = lax.broadcasted_iota(jnp.int32, heads, 0) // rows == lax.broadcasted_iota(
        jnp.int32, heads, 1
    )
    sink = jnp.sum(jnp.where(of_head, sink_ref[...], 0.0), axis=1, keepdims=True)
    newest = jnp.sum(stacked * new_all, axis=1, keepdims=True)
    is_new = lanes == (pos & (window - 1))
    scores = jnp.where(is_new, newest, scores) * (half**-0.5)
    scores = jnp.where(lanes <= pos, scores, -jnp.inf)
    largest = jnp.maximum(jnp.max(scores, axis=1, keepdims=True), sink)
    raised = jnp.exp(scores - largest)
    total = jnp.sum(raised, axis=1, keepdims=True) + jnp.exp(sink - largest)
    weights = (raised / total).astype(jnp.bfloat16).astype(jnp.float32)
    newest_weight = jnp.sum(jnp.where(is_new, weights, 0.0), axis=1, keepdims=True)
    older = jnp.where(is_new, 0.0, weights)
    spread = jnp.concatenate(
        [jnp.where(request == t, older, 0.0).astype(jnp.bfloat16) for t in range(rows)], axis=1
    )
    mixed = jnp.dot(spread, kv, preferred_element_type=jnp.float32)
    mixed = mixed + newest_weight * new_all
    merged = []
    for pair in range(groups // 2):
        even = mixed[2 * pair * rows : (2 * pair + 1) * rows]
        odd = mixed[(2 * pair + 1) * rows : (2 * pair + 2) * rows]
        merged.append(jnp.where(low, pltpu.roll(even, half, 1), odd))
    merged = jnp.concatenate(merged, axis=1).astype(jnp.bfloat16)
    proj_copy.wait()
    for s in range(shares):
        out_ref[s] = lax.dot_general(
            merged,
            proj_ref[pl.ds(s * share_width, share_width), :],
            (((1,), (1,)), ((), ())),
            preferred_element_type=jnp.float32,
        ).astype(jnp.bfloat16)


def attend(positions, sink_logits, queries, kv_cache, new_kv, out_proj):
    rows, _, window, width = kv_cache.shape
    features = out_proj.shape[2]
    hbm = pl.BlockSpec(memory_space=pltpu.HBM)
    return pl.pallas_call(
        attend_kernel,
        out_shape=pltpu.VMEM((8, rows, features // 8), jnp.bfloat16),
        in_specs=[hbm] * 6,
        out_specs=pl.BlockSpec(memory_space=pltpu.VMEM),
        scratch_shapes=[
            pltpu.VMEM((1, rows), jnp.int32),
            pltpu.VMEM(sink_logits.shape, jnp.float32),
            pltpu.VMEM((rows, queries.shape[2]), jnp.bfloat16),
            pltpu.VMEM((rows, window, width), jnp.bfloat16),
            pltpu.VMEM((rows, width), jnp.bfloat16),
            pltpu.VMEM((features, out_proj.shape[1]), jnp.bfloat16),
            pltpu.SemaphoreType.DMA((6,)),
        ],
        compiler_params=pltpu.CompilerParams(vmem_limit_bytes=16 * MIB),
        name="attend",
    )(
        *(
            pltpu.with_memory_space_constraint(x, pltpu.HBM)
            for x in (
                positions.reshape(1, rows),
                sink_logits,
                queries.reshape(rows, -1),
                kv_cache.reshape(rows, window, width),
                new_kv.reshape(rows, width),
                jnp.swapaxes(out_proj[0], 0, 1),
            )
        )
    )


def dispatch_kernel(
    parts_ref,
    ids_ref,
    scale_ref,
    resid_ref,
    gain_ref,
    later_hbm,
    hidden_ref,
    out_ref,
    combine_ref,
    share_ref,
    gain_here_ref,
    row_ref,
):
    rows, share_width = hidden_ref.shape
    gain = gain_ref[...][None, :]
    here = 2 * lax.axis_index("y") + lax.axis_index("core")
    for s in range(parts_ref.shape[0]):

        @pl.when(here == s)
        def _(s=s):
            share_ref[...] = resid_ref[:, s * share_width : (s + 1) * share_width]
            gain_here_ref[...] = gain[:, s * share_width : (s + 1) * share_width]

    line = lax.broadcasted_iota(jnp.int32, combine_ref.shape, 0)
    named = jnp.zeros(combine_ref.shape, jnp.float32)
    weighted = jnp.zeros(combine_ref.shape, jnp.float32)
    for k in range(ids_ref.shape[0]):
        match = ids_ref[k : k + 1, :] == line // 2
        named = jnp.where(match, 1.0, named)
        weighted = jnp.where(
            match, scale_ref[k : k + 1, :].astype(jnp.float32) / 65536.0, weighted
        )
    square = (rows, rows)
    ahead = lax.broadcasted_iota(jnp.int32, square, 0) < lax.broadcasted_iota(
        jnp.int32, square, 1
    )
    before = jnp.dot(
        named, ahead.astype(jnp.float32), preferred_element_type=jnp.float32
    ).astype(jnp.int32)
    kept = before == line % 2
    combine_ref[...] = jnp.where(kept, weighted, 0.0)
    pick = jnp.where(kept, named, 0.0).astype(jnp.bfloat16)

    summed = jnp.sum(parts_ref[...].astype(jnp.float32), axis=0)
    hidden = (share_ref[...].astype(jnp.float32) + summed).astype(jnp.bfloat16)
    hidden_ref[...] = hidden
    wide = hidden.astype(jnp.float32)
    squares = jnp.sum(wide * wide, axis=1, keepdims=True)
    high = squares.astype(jnp.bfloat16).astype(jnp.float32)
    rest = (rows, row_ref.shape[1] - share_width)
    lane = lax.broadcasted_iota(jnp.int32, rest, 1)
    row_ref[:, :share_width] = (wide * gain_here_ref[...]).astype(jnp.bfloat16)
    row_ref[:, share_width:] = jnp.where(
        lane == 0, high, jnp.where(lane == 1, squares - high, 0.0)
    ).astype(jnp.bfloat16)
    out_ref[...] = jnp.dot(
        pick, row_ref[...], preferred_element_type=jnp.float32
    ).astype(jnp.bfloat16)


def swap_rows(rows, outer, inner):
    count = rows.shape[0]
    to = lax.broadcasted_iota(jnp.int32, (count, count), 0)
    at = lax.broadcasted_iota(jnp.int32, (count, count), 1)
    source = ((to // 2) % outer) * (2 * inner) + (to // (2 * outer)) * 2 + to % 2
    return jnp.dot(
        (at == source).astype(jnp.bfloat16), rows, preferred_element_type=jnp.float32
    ).astype(jnp.bfloat16)


def spread_kernel(got_ref, out_ref):
    rows = swap_rows(got_ref[...], GRID[0], GRID[1])
    for y in range(out_ref.shape[0]):
        out_ref[y] = rows


def gather_kernel(parts_ref, out_ref):
    z_size, x_size = GRID[0], GRID[1]
    share = out_ref.shape[1]
    summed = jnp.sum(parts_ref[...].astype(jnp.float32), axis=0)[:, :share]
    out_ref[...] = swap_rows(summed.astype(jnp.bfloat16), x_size, z_size)


def relay_kernel(up_ref, down_hbm, up_out, down_out, down_ref, sem):
    copy = pltpu.make_async_copy(down_hbm, down_ref, sem)
    copy.start()
    y_size = GRID[2]
    share = down_ref.shape[1] // (2 * y_size)
    lanes = down_out.shape[1] // y_size
    up = up_ref[...]
    rest = jnp.zeros((up.shape[0], lanes - share), jnp.bfloat16)
    for y in range(y_size):
        for c in range(2):
            start = (2 * y + c) * share
            up_out[c, :, y * lanes : y * lanes + share] = up[:, start : start + share]
            up_out[c, :, y * lanes + share : (y + 1) * lanes] = rest
    copy.wait()
    for c in range(2):

        @pl.when(lax.axis_index("core") == c)
        def _(c=c):
            for y in range(y_size):
                start = (2 * y + 1 - c) * share
                down_out[:, y * lanes : y * lanes + share] = down_ref[:, start : start + share]
                down_out[:, y * lanes + share : (y + 1) * lanes] = jnp.zeros(
                    (down_ref.shape[0], lanes - share), jnp.bfloat16
                )


def joined(ref):
    return jnp.concatenate([ref[y] for y in range(ref.shape[0])], axis=1)


def expert_kernel(mine_ref, theirs_ref, up_ref, down_ref, act_ref, send_ref, held_ref):
    core = lax.axis_index("core")
    y_size, slots, lanes = mine_ref.shape
    share = FEATURES // (2 * y_size)
    units = act_ref.shape[0]
    projected = jnp.zeros(held_ref.shape, jnp.float32)
    squares = jnp.zeros((slots, 128), jnp.float32)
    for ref, index in ((mine_ref, core), (theirs_ref, 1 - core)):
        projected = projected + lax.dot_general(
            up_ref[index], joined(ref), (((1,), (1,)), ((), ())), preferred_element_type=jnp.float32
        )
        for y in range(y_size):
            squares = squares + ref[y, :, lanes - 128 :].astype(jnp.float32)
    place = lax.broadcasted_iota(jnp.int32, squares.shape, 1) + (lanes - 128 - share)
    squares = jnp.where((place == 0) | (place == 1), squares, 0.0)
    mean_square = jnp.sum(jnp.transpose(squares), axis=0, keepdims=True) / FEATURES
    held_ref[...] = projected * lax.rsqrt(mean_square + epsilon)
    gate = held_ref[pl.ds(0, units, stride=2), :]
    up = held_ref[pl.ds(1, units, stride=2), :]
    act = ((up + 1.0) * gate * jax.nn.sigmoid(swish_alpha * gate)).astype(jnp.bfloat16)
    act_ref[...] = act
    partial = lax.dot_general(
        act, down_ref[...], (((0,), (0,)), ((), ())), preferred_element_type=jnp.float32
    ).astype(jnp.bfloat16)
    for y in range(y_size):
        send_ref[y] = partial[:, y * lanes : (y + 1) * lanes]


def own_kernel(act_ref, down_ref, combine_ref, out_ref, halves_ref):
    y_size = out_ref.shape[0]
    combine = jnp.transpose(combine_ref[...])
    rows = combine.shape[0]
    high = combine.astype(jnp.bfloat16)
    halves_ref[:rows] = high
    halves_ref[rows:] = (combine - high.astype(jnp.float32)).astype(jnp.bfloat16)
    share = down_ref.shape[1] // (2 * y_size)
    partial = lax.dot_general(
        act_ref[...], down_ref[...], (((0,), (0,)), ((), ())), preferred_element_type=jnp.float32
    )
    for c in range(2):

        @pl.when(lax.axis_index("core") == c)
        def _(c=c):
            for y in range(y_size):
                start = (2 * y + c) * share
                out_ref[y, :, :share] = partial[:, start : start + share]


def finish_kernel(hidden_ref, halves_ref, back_ref, out_ref):
    rows = hidden_ref.shape[0]
    mixed = jnp.dot(halves_ref[...], back_ref[...], preferred_element_type=jnp.float32)
    mixture = mixed[:rows] + mixed[rows:]
    out_ref[...] = (hidden_ref[...].astype(jnp.float32) + mixture).astype(jnp.bfloat16)


def run(kernel, name, outs, scratch=(), from_hbm=()):
    vmem = pl.BlockSpec(memory_space=pltpu.VMEM)
    hbm = pl.BlockSpec(memory_space=pltpu.HBM)

    def call(*operands):
        return pl.pallas_call(
            kernel,
            out_shape=tuple(pltpu.VMEM(shape, dtype) for shape, dtype in outs),
            in_specs=[hbm if i in from_hbm else vmem for i in range(len(operands))],
            out_specs=(vmem,) * len(outs),
            scratch_shapes=list(scratch),
            compiler_params=pltpu.CompilerParams(vmem_limit_bytes=16 * MIB),
            name=name,
        )(*operands)

    return call


def local(
    residual,
    queries,
    kv_cache,
    new_kv,
    positions,
    sink_logits,
    out_proj,
    norm_gain,
    route_ids,
    route_weights,
    w_gate_up,
    w_down,
):
    rows, features = residual.shape
    z_size, x_size, y_size, _ = GRID
    share = features // (2 * y_size)
    lanes = pl.cdiv(share, 128) * 128
    slots = 2 * z_size * x_size
    units = w_down.shape[1]
    bf16 = jnp.bfloat16
    swap = [(0, 1), (1, 0)]

    parts = attend(positions, sink_logits, queries, kv_cache, new_kv, out_proj)
    parts = lax.all_to_all(parts, HEAD, 0, 0, tiled=True)
    gate_up = jnp.swapaxes(w_gate_up[0], 0, 1)
    hidden, outgoing, combine = run(
        dispatch_kernel,
        "dispatch",
        [((rows, share), bf16), ((slots, lanes), bf16), ((slots, rows), jnp.float32)],
        [
            pltpu.VMEM((rows, share), bf16),
            pltpu.VMEM((1, share), jnp.float32),
            pltpu.VMEM((rows, lanes), bf16),
        ],
        from_hbm=(5,),
    )(
        parts,
        route_ids.T,
        route_weights.T,
        residual,
        norm_gain,
        pltpu.with_memory_space_constraint(gate_up, pltpu.HBM),
    )

    got = lax.all_to_all(outgoing.reshape(z_size, 2 * x_size, lanes), "z", 0, 0, tiled=True)
    (spread,) = run(spread_kernel, "spread", [((y_size, slots, lanes), bf16)])(
        got.reshape(slots, lanes)
    )
    mine = lax.all_to_all(
        spread.reshape(y_size * x_size, 2 * z_size, lanes), PLANE, 0, 0, tiled=True
    ).reshape(y_size, slots, lanes)
    gate_up, down, mine = lax.optimization_barrier((gate_up, w_down[0], mine))
    gate_up, sent_down = run(
        relay_kernel,
        "relay",
        [((2, 2 * units, y_size * lanes), bf16), ((units, y_size * lanes), bf16)],
        [pltpu.VMEM((units, features), bf16), pltpu.SemaphoreType.DMA],
        from_hbm=(1,),
    )(gate_up, pltpu.with_memory_space_constraint(down, pltpu.HBM))
    theirs = lax.ppermute(mine, "core", swap)
    act, sent = run(
        expert_kernel,
        "expert",
        [((units, slots), bf16), ((y_size, slots, lanes), bf16)],
        [pltpu.VMEM((2 * units, slots), jnp.float32)],
    )(mine, theirs, gate_up, sent_down)

    arrived = lax.ppermute(sent, "core", swap)
    own, halves = run(
        own_kernel,
        "own",
        [((y_size, slots, lanes), jnp.float32), ((2 * rows, slots), bf16)],
    )(act, down, combine)
    paired = (own + arrived.astype(jnp.float32)).astype(bf16)
    paired = lax.all_to_all(
        paired.reshape(y_size * x_size, 2 * z_size, lanes), PLANE, 0, 0, tiled=True
    )
    (summed,) = run(gather_kernel, "gather", [((slots, share), bf16)])(
        paired.reshape(y_size, slots, lanes)
    )
    back = lax.all_to_all(summed.reshape(z_size, 2 * x_size, share), "z", 0, 0, tiled=True)
    return pl.pallas_call(
        finish_kernel,
        out_shape=jax.ShapeDtypeStruct((rows, share), bf16),
        in_specs=[pl.BlockSpec(memory_space=pltpu.VMEM)] * 3,
        out_specs=pl.BlockSpec(memory_space=pltpu.VMEM),
        compiler_params=pltpu.CompilerParams(vmem_limit_bytes=16 * MIB),
        name="finish",
    )(hidden, halves, back.reshape(slots, share))


def solution(mesh):
    fine = Mesh(mesh.devices.reshape(GRID), ("z", "x", "y", "core"))
    in_specs = (
        P(GRP, None),
        P(GRP, HEAD, None),
        P(GRP, HEAD, None, None),
        P(GRP, HEAD, None),
        P(GRP),
        P(HEAD, None),
        P(HEAD, None, None),
        P(),
        P(GRP, None),
        P(GRP, None),
        P(GRP, None, HEAD),
        P(GRP, HEAD, None),
    )
    return jax.shard_map(
        local, mesh=fine, in_specs=in_specs, out_specs=P(GRP, HEAD), check_vma=False
    )
```

time: 96.3 us -> 95.2 us (0.989)
    pallas_call x1 -> x2, Pallas kernels: 3.65 us -> 3.25 us  [the longest x1 2.51 us: attend(): pl.pallas_call(attend_kernel, out_shape=pltpu.VMEM((8, rows, features //...]
  transfers between devices with their start and end apart: 2 -> 2, of which waited for: 1 -> 2; matrix products, arithmetic and copies ran while one was open for 0% -> 0% of each run, Pallas kernels for 2% -> 2%
where the time goes in v4:
time: 95.2 us; the launch traced here: 94.8 us
  blocking collectives  82.1 us (86%)
  Pallas kernels  7.41 us (8%)
  starting transfers between devices  4.15 us (4%)
    all_to_all x1, blocking collectives, local(): lax.all_to_all(outgoing.reshape(z_size, 2 * x_size, lanes), 'z', 0, 0, ti...  27.7 us
    all_to_all x1, blocking collectives, local(): lax.all_to_all(summed.reshape(z_size, 2 * x_size, share), 'z', 0, 0, tile...  16.5 us
    all_to_all x1, blocking collectives, local(): lax.all_to_all(spread.reshape(y_size * x_size, 2 * z_size, lanes), PLANE,...  14.2 us
    all_to_all x1, blocking collectives, local(): lax.all_to_all(paired.reshape(y_size * x_size, 2 * z_size, lanes), PLANE,...  13.5 us
    all_to_all x1, blocking collectives, local(): parts = lax.all_to_all(parts, HEAD, 0, 0, tiled=True)  10.2 us
    pallas_call x6, Pallas kernels, call(): pl.pallas_call(kernel, out_shape=tuple((pltpu.VMEM(shape, dtype) for shap...  4.16 us
    pallas_call x1, Pallas kernels, attend(): pl.pallas_call(attend_kernel, out_shape=pltpu.VMEM((8, rows, features //...  2.51 us
    ppermute x1, starting transfers between devices, local(): arrived = lax.ppermute(sent, 'core', swap)  2.24 us
  transfers between devices with their start and end apart: 2, of which 2 were waited for; matrix products, arithmetic and copies ran while one was open for 0% of the time, Pallas kernels for 2%

profile of v4, /device:TPU:32, one launch (start us, length us, event | category | flops | bytes accessed | tf_op | source)
XLA Modules:
  0.0 94.8 jit_solution(3828196288834497013)
XLA Ops:
  0.0 0.0 copy-start.2
  0.0 2.5 %attend.1 = bf16[8,16,360]{2,1,0:T(8,128)(2,1)S(1)} custom-call(s32[1,16]{1,0:T(1,128)} %bitcast.40, f32[1,4]{1,0:T(1,128)} %sink_hbm.1, bf16[16,256]{1,0:T(8,128)(2,1)} %bitcast.38, bf16[16,128,128]{2,1,0:T(8,128)(2,1)} %bitcast.37, bf16[16,128]{1,0:T(8,128)(2,1)} %bitcast.39, bf16[2880,256]{1,0:T(8,128)(2,1)} %bitcast.36), custom_call_target="tpu_custom_call" | custom-call | tf_op jit(solution)/shard_map/attend/pallas_call | solution.py:128
  2.5 0.0 copy-start
  2.6 10.2 %all_to_all.25.parts_ref = bf16[8,16,360]{2,1,0:T(8,128)(2,1)S(1)} all-to-all(bf16[8,16,360]{2,1,0:T(8,128)(2,1)S(1)} %attend.1), channel_id=1, replica_groups=mesh['z'=16,'x'=4,'y'=4,'core'=2] {'y','core'}, dimensions={0} | all-to-all | bytes 184320 | tf_op jit(solution)/shard_map/all_to_all | solution.py:370
  12.8 0.0 copy-done.5
  12.8 0.0 copy-done.4
  12.8 0.4 dispatch.1
  13.1 27.7 %all_to_all.26 = bf16[16,8,384]{2,1,0:T(8,128)(2,1)S(1)} all-to-all(bf16[16,8,384]{2,1,0:T(8,128)(2,1)S(1)} %bitcast.32), channel_id=1, replica_groups=mesh['z'=16,'x'=4,'y'=4,'core'=2] {'z'}, dimensions={0} | all-to-all | bytes 196608 | tf_op jit(solution)/shard_map/all_to_all | solution.py:391
  40.9 0.2 spread.1
  41.0 14.2 %all_to_all.27 = bf16[16,32,384]{2,1,0:T(8,128)(2,1)S(1)} all-to-all(bf16[16,32,384]{2,1,0:T(8,128)(2,1)S(1)} %bitcast.27), channel_id=1, replica_groups=mesh['z'=16,'x'=4,'y'=4,'core'=2] {'y','x'}, dimensions={0} | all-to-all | bytes 786432 | tf_op jit(solution)/shard_map/all_to_all | solution.py:395
  55.3 1.9 %collective-permute-start = (bf16[4,128,384]{2,1,0:T(8,128)(2,1)S(1)}, bf16[4,128,384]{2,1,0:T(8,128)(2,1)S(1)}, u32[]{:S(2)}, u32[]{:S(2)}) collective-permute-start(bf16[4,128,384]{2,1,0:T(8,128)(2,1)S(1)} %bitcast.25), channel_id=1, source_target_pairs={{0,1},{1,0},{2,3},{3,2},{4,5},{5,4},{6,7},{7,6},{8,9},{9,8},{10,11... | collective-permute-start | bytes 1179656 | tf_op jit(solution)/shard_map/ppermute | solution.py:406
  57.2 1.5 %relay.1 = (bf16[2,360,1536]{2,1,0:T(8,128)(2,1)S(1)}, bf16[180,1536]{1,0:T(8,128)(2,1)S(1)}) custom-call(bf16[360,2880]{1,0:T(8,128)(2,1)S(1)} %bitcast.22, bf16[180,2880]{1,0:T(8,128)(2,1)} %bitcast.23), custom_call_target="tpu_custom_call" | custom-call | tf_op jit(solution)/shard_map/relay/pallas_call | solution.py:333
  58.8 0.0 copy-start.1
  58.8 0.1 collective-permute-done.theirs_ref
  58.9 1.3 %expert.1 = (bf16[180,128]{1,0:T(8,128)(2,1)S(1)}, bf16[4,128,384]{2,1,0:T(8,128)(2,1)S(1)}) custom-call(bf16[4,128,384]{2,1,0:T(8,128)(2,1)S(1)} %bitcast.26, bf16[4,128,384]{2,1,0:T(8,128)(2,1)S(1)} %collective-permute-done.theirs_ref, bf16[2,360,1536]{2,1,0:T(8,128)(2,1)S(1)} %get-tuple-element.22.up_ref, bf16[180,1536]{1,0:T(8,128)(2,1)S(1)} %get-tuple-element.23.down_ref), custom_call_target="tpu_custom_call" | custom-call | tf_op jit(solution)/shard_map/expert/pallas_call | solution.py:333
  60.2 2.2 %collective-permute-start.1 = (bf16[4,128,384]{2,1,0:T(8,128)(2,1)S(1)}, bf16[4,128,384]{2,1,0:T(8,128)(2,1)S(1)}, u32[]{:S(2)}, u32[]{:S(2)}) collective-permute-start(bf16[4,128,384]{2,1,0:T(8,128)(2,1)S(1)} %get-tuple-element.28), channel_id=1, source_target_pairs={{0,1},{1,0},{2,3},{3,2},{4,5},{5,4},{6,7},{7,6},{8,9},{9,8},{10,11... | collective-permute-start | bytes 1179656 | tf_op jit(solution)/shard_map/ppermute | solution.py:414
  62.4 0.0 copy-done.1
  62.4 0.6 own.1
  63.1 0.7 collective-permute-done.1
  63.8 0.1 add_convert_fusion
  63.9 13.5 %all_to_all.28 = bf16[16,32,384]{2,1,0:T(8,128)(2,1)S(1)} all-to-all(bf16[16,32,384]{2,1,0:T(8,128)(2,1)S(1)} %bitcast.35), channel_id=1, replica_groups=mesh['z'=16,'x'=4,'y'=4,'core'=2] {'y','x'}, dimensions={0} | all-to-all | bytes 786432 | tf_op jit(solution)/shard_map/all_to_all | solution.py:421
  77.4 0.2 gather.1
  77.6 16.5 %all_to_all.29 = bf16[16,8,360]{2,1,0:T(8,128)(2,1)S(1)} all-to-all(bf16[16,8,360]{2,1,0:T(8,128)(2,1)S(1)} %bitcast.31), channel_id=1, replica_groups=mesh['z'=16,'x'=4,'y'=4,'core'=2] {'z'}, dimensions={0} | all-to-all | bytes 184320 | tf_op jit(solution)/shard_map/all_to_all | solution.py:427
  94.1 0.7 finish.1
  (6 shorter events, 0.0 us)
Async XLA Ops:
  0.0 12.8 %copy-start.5 = (s32[16,4]{0,1:T(4,128)S(1)}, s32[16,4]{0,1:T(4,128)}, u32[]{:S(2)}) copy-start(s32[16,4]{0,1:T(4,128)} %param.21) | copy-start | bytes 772
  0.0 12.8 %copy-start.4 = (s32[16,4]{0,1:T(4,128)S(1)}, s32[16,4]{0,1:T(4,128)}, u32[]{:S(2)}) copy-start(s32[16,4]{0,1:T(4,128)} %param.20) | copy-start | bytes 772
  0.0 12.8 %copy-start.3 = (f32[2880]{0:T(1024)S(1)}, f32[2880]{0:T(1024)}, u32[]{:S(2)}) copy-start(f32[2880]{0:T(1024)} %gain_ref.1) | copy-start | bytes 34564
  0.0 12.8 %copy-start.2 = (bf16[16,2880]{1,0:T(8,128)(2,1)S(1)}, bf16[16,2880]{1,0:T(8,128)(2,1)}, u32[]{:S(2)}) copy-start(bf16[16,2880]{1,0:T(8,128)(2,1)} %resid_ref.1) | copy-start | bytes 276484
  2.5 54.7 %copy-start = (bf16[1,2880,360]{1,2,0:T(8,128)(2,1)S(1)}, bf16[1,2880,360]{1,2,0:T(8,128)(2,1)}, u32[]{:S(2)}) copy-start(bf16[1,2880,360]{1,2,0:T(8,128)(2,1)} %param.22) | copy-start | bytes 6220804
  55.3 3.6 %collective-permute-start = (bf16[4,128,384]{2,1,0:T(8,128)(2,1)S(1)}, bf16[4,128,384]{2,1,0:T(8,128)(2,1)S(1)}, u32[]{:S(2)}, u32[]{:S(2)}) collective-permute-start(bf16[4,128,384]{2,1,0:T(8,128)(2,1)S(1)} %bitcast.25), channel_id=1, source_target_pairs={{0,1},{1,0},{2,3},{3,2},{4,5},{5,4},{6,7},{7,6},{8,9},{9,8},{10,11... | collective-permute-start | bytes 1179656 | tf_op jit(solution)/shard_map/ppermute | solution.py:406
  58.8 3.7 %copy-start.1 = (bf16[1,180,2880]{2,1,0:T(8,128)(2,1)S(1)}, bf16[1,180,2880]{2,1,0:T(8,128)(2,1)}, u32[]{:S(2)}) copy-start(bf16[1,180,2880]{2,1,0:T(8,128)(2,1)} %param.23) | copy-start | bytes 3110404
  60.2 3.6 %collective-permute-start.1 = (bf16[4,128,384]{2,1,0:T(8,128)(2,1)S(1)}, bf16[4,128,384]{2,1,0:T(8,128)(2,1)S(1)}, u32[]{:S(2)}, u32[]{:S(2)}) collective-permute-start(bf16[4,128,384]{2,1,0:T(8,128)(2,1)S(1)} %get-tuple-element.28), channel_id=1, source_target_pairs={{0,1},{1,0},{2,3},{3,2},{4,5},{5,4},{6,7},{7,6},{8,9},{9,8},{10,11... | collective-permute-start | bytes 1179656 | tf_op jit(solution)/shard_map/ppermute | solution.py:414

commit v5 on v4

--- a/solution.py
+++ b/solution.py
@@ -5,6 +5,7 @@
 from jax.experimental.pallas import tpu as pltpu
 from jax.sharding import Mesh, PartitionSpec as P
 
+
 epsilon = 1e-05
 swish_alpha = 1.702
 
@@ -13,6 +14,7 @@
 HEAD = ("y", "core")
 PLANE = ("y", "x")
 FEATURES = 2880
+DOWN_AT = 368
 MIB = 1 << 20
 
 
@@ -240,82 +242,109 @@
     out_ref[...] = swap_rows(summed.astype(jnp.bfloat16), x_size, z_size)
 
 
-def relay_kernel(up_ref, down_hbm, up_out, down_out, down_ref, sem):
-    copy = pltpu.make_async_copy(down_hbm, down_ref, sem)
-    copy.start()
+def lay(source, out, first, c):
     y_size = GRID[2]
-    share = down_ref.shape[1] // (2 * y_size)
-    lanes = down_out.shape[1] // y_size
-    up = up_ref[...]
-    rest = jnp.zeros((up.shape[0], lanes - share), jnp.bfloat16)
+    share = source.shape[1] // (2 * y_size)
+    lanes = out.shape[1] // y_size
+    count = source.shape[0]
+    at = pl.ds(first, count)
     for y in range(y_size):
-        for c in range(2):
-            start = (2 * y + c) * share
-            up_out[c, :, y * lanes : y * lanes + share] = up[:, start : start + share]
-            up_out[c, :, y * lanes + share : (y + 1) * lanes] = rest
-    copy.wait()
+        start = (2 * y + c) * share
+        out[at, y * lanes : y * lanes + share] = source[:, start : start + share]
+        out[at, y * lanes + share : (y + 1) * lanes] = jnp.zeros(
+            (count, lanes - share), jnp.bfloat16
+        )
+
+
+def for_core(act):
     for c in range(2):
 
         @pl.when(lax.axis_index("core") == c)
         def _(c=c):
-            for y in range(y_size):
-                start = (2 * y + 1 - c) * share
-                down_out[:, y * lanes : y * lanes + share] = down_ref[:, start : start + share]
-                down_out[:, y * lanes + share : (y + 1) * lanes] = jnp.zeros(
-                    (down_ref.shape[0], lanes - share), jnp.bfloat16
-                )
-
-
-def joined(ref):
-    return jnp.concatenate([ref[y] for y in range(ref.shape[0])], axis=1)
-
-
-def expert_kernel(mine_ref, theirs_ref, up_ref, down_ref, act_ref, send_ref, held_ref):
-    core = lax.axis_index("core")
-    y_size, slots, lanes = mine_ref.shape
-    share = FEATURES // (2 * y_size)
-    units = act_ref.shape[0]
-    projected = jnp.zeros(held_ref.shape, jnp.float32)
-    squares = jnp.zeros((slots, 128), jnp.float32)
-    for ref, index in ((mine_ref, core), (theirs_ref, 1 - core)):
-        projected = projected + lax.dot_general(
-            up_ref[index], joined(ref), (((1,), (1,)), ((), ())), preferred_element_type=jnp.float32
-        )
-        for y in range(y_size):
-            squares = squares + ref[y, :, lanes - 128 :].astype(jnp.float32)
-    place = lax.broadcasted_iota(jnp.int32, squares.shape, 1) + (lanes - 128 - share)
-    squares = jnp.where((place == 0) | (place == 1), squares, 0.0)
-    mean_square = jnp.sum(jnp.transpose(squares), axis=0, keepdims=True) / FEATURES
-    held_ref[...] = projected * lax.rsqrt(mean_square + epsilon)
-    gate = held_ref[pl.ds(0, units, stride=2), :]
-    up = held_ref[pl.ds(1, units, stride=2), :]
-    act = ((up + 1.0) * gate * jax.nn.sigmoid(swish_alpha * gate)).astype(jnp.bfloat16)
-    act_ref[...] = act
-    partial = lax.dot_general(
-        act, down_ref[...], (((0,), (0,)), ((), ())), preferred_element_type=jnp.float32
-    ).astype(jnp.bfloat16)
-    for y in range(y_size):
-        send_ref[y] = partial[:, y * lanes : (y + 1) * lanes]
-
-
-def own_kernel(act_ref, down_ref, combine_ref, out_ref, halves_ref):
-    y_size = out_ref.shape[0]
+            act(c)
+
+
+def relay_kernel(
+    up_ref, down_hbm, combine_ref, up_out, send_hbm, halves_ref, send_ref, down_ref, sems
+):
+    copy = pltpu.make_async_copy(down_hbm, down_ref, sems.at[0])
+    copy.start()
+    for_core(lambda c: lay(up_ref[...], send_ref, 0, 1 - c))
+    top = pltpu.make_async_copy(
+        send_ref.at[pl.ds(0, DOWN_AT)], send_hbm.at[pl.ds(0, DOWN_AT)], sems.at[1]
+    )
+    top.start()
+    for_core(lambda c: lay(up_ref[...], up_out, 0, c))
     combine = jnp.transpose(combine_ref[...])
     rows = combine.shape[0]
     high = combine.astype(jnp.bfloat16)
     halves_ref[:rows] = high
     halves_ref[rows:] = (combine - high.astype(jnp.float32)).astype(jnp.bfloat16)
-    share = down_ref.shape[1] // (2 * y_size)
-    partial = lax.dot_general(
-        act_ref[...], down_ref[...], (((0,), (0,)), ((), ())), preferred_element_type=jnp.float32
-    )
-    for c in range(2):
-
-        @pl.when(lax.axis_index("core") == c)
-        def _(c=c):
-            for y in range(y_size):
-                start = (2 * y + c) * share
-                out_ref[y, :, :share] = partial[:, start : start + share]
+    copy.wait()
+    for_core(lambda c: lay(down_ref[...], send_ref, DOWN_AT, 1 - c))
+    rest = send_ref.shape[0] - DOWN_AT
+    bottom = pltpu.make_async_copy(
+        send_ref.at[pl.ds(DOWN_AT, rest)], send_hbm.at[pl.ds(DOWN_AT, rest)], sems.at[2]
+    )
+    bottom.start()
+    top.wait()
+    bottom.wait()
+
+
+def keep_kernel(down_hbm, after_ref, out_ref, down_ref, sem):
+    copy = pltpu.make_async_copy(down_hbm, down_ref, sem)
+    copy.start()
+    copy.wait()
+    for_core(lambda c: lay(down_ref[...], out_ref, 0, c))
+
+
+def joined(ref):
+    return jnp.concatenate([ref[y] for y in range(ref.shape[0])], axis=1)
+
+
+def project_kernel(mine_ref, up_ref, partner_ref, out_ref):
+    y_size, slots, lanes = mine_ref.shape
+    share = FEATURES // (2 * y_size)
+    columns = up_ref.shape[0]
+    x = joined(mine_ref)
+    for block, ref in enumerate((up_ref, partner_ref)):
+        out_ref[pl.ds(block * columns, columns), :] = lax.dot_general(
+            ref[pl.ds(0, columns), :],
+            x,
+            (((1,), (1,)), ((), ())),
+            preferred_element_type=jnp.float32,
+        )
+    squares = jnp.zeros((slots, 128), jnp.float32)
+    for y in range(y_size):
+        squares = squares + mine_ref[y, :, lanes - 128 :].astype(jnp.float32)
+    place = lax.broadcasted_iota(jnp.int32, squares.shape, 1) + (lanes - 128 - share)
+    squares = jnp.where((place == 0) | (place == 1), squares, 0.0)
+    squares = jnp.sum(jnp.transpose(squares), axis=0, keepdims=True)
+    tail = out_ref.shape[0] - 2 * columns
+    out_ref[pl.ds(2 * columns, tail), :] = jnp.broadcast_to(squares, (tail, slots))
+
+
+def down_kernel(here_ref, there_ref, down_ref, partner_ref, out_ref, held_ref):
+    units = down_ref.shape[0]
+    columns = 2 * units
+    y_size, _, lanes = out_ref.shape
+    last = here_ref.shape[0] - 1
+    squares = here_ref[last : last + 1, :] + there_ref[last : last + 1, :]
+    scale = lax.rsqrt(squares / FEATURES + epsilon)
+    total = jnp.zeros((out_ref.shape[1], y_size * lanes), jnp.float32)
+    for block, weights in enumerate((down_ref[...], partner_ref[pl.ds(DOWN_AT, units), :])):
+        held_ref[block] = (
+            here_ref[pl.ds(block * columns, columns), :]
+            + there_ref[pl.ds((1 - block) * columns, columns), :]
+        ) * scale
+        gate = held_ref[block, pl.ds(0, units, stride=2), :]
+        up = held_ref[block, pl.ds(1, units, stride=2), :]
+        act = ((up + 1.0) * gate * jax.nn.sigmoid(swish_alpha * gate)).astype(jnp.bfloat16)
+        total = total + lax.dot_general(
+            act, weights, (((0,), (0,)), ((), ())), preferred_element_type=jnp.float32
+        )
+    for y in range(y_size):
+        out_ref[y] = total[:, y * lanes : (y + 1) * lanes].astype(jnp.bfloat16)
 
 
 def finish_kernel(hidden_ref, halves_ref, back_ref, out_ref):
@@ -325,7 +354,7 @@
     out_ref[...] = (hidden_ref[...].astype(jnp.float32) + mixture).astype(jnp.bfloat16)
 
 
-def run(kernel, name, outs, scratch=(), from_hbm=()):
+def run(kernel, outs, scratch=(), from_hbm=()):
     vmem = pl.BlockSpec(memory_space=pltpu.VMEM)
     hbm = pl.BlockSpec(memory_space=pltpu.HBM)
 
@@ -337,7 +366,6 @@
             out_specs=(vmem,) * len(outs),
             scratch_shapes=list(scratch),
             compiler_params=pltpu.CompilerParams(vmem_limit_bytes=16 * MIB),
-            name=name,
         )(*operands)
 
     return call
@@ -371,7 +399,6 @@
     gate_up = jnp.swapaxes(w_gate_up[0], 0, 1)
     hidden, outgoing, combine = run(
         dispatch_kernel,
-        "dispatch",
         [((rows, share), bf16), ((slots, lanes), bf16), ((slots, rows), jnp.float32)],
         [
             pltpu.VMEM((rows, share), bf16),
@@ -388,42 +415,58 @@
         pltpu.with_memory_space_constraint(gate_up, pltpu.HBM),
     )
 
+    outgoing, gate_up, down = lax.optimization_barrier((outgoing, gate_up, w_down[0]))
+    down = pltpu.with_memory_space_constraint(down, pltpu.HBM)
+    width = y_size * lanes
+    sent_rows = DOWN_AT + pl.cdiv(units, 16) * 16
+    vmem = pl.BlockSpec(memory_space=pltpu.VMEM)
+    hbm = pl.BlockSpec(memory_space=pltpu.HBM)
+    gate_up, to_partner, halves = pl.pallas_call(
+        relay_kernel,
+        out_shape=(
+            pltpu.VMEM((2 * units, width), bf16),
+            pltpu.HBM((sent_rows, width), bf16),
+            pltpu.VMEM((2 * rows, slots), bf16),
+        ),
+        in_specs=[vmem, hbm, vmem],
+        out_specs=(vmem, hbm, vmem),
+        scratch_shapes=[
+            pltpu.VMEM((sent_rows, width), bf16),
+            pltpu.VMEM((units, features), bf16),
+            pltpu.SemaphoreType.DMA((3,)),
+        ],
+        compiler_params=pltpu.CompilerParams(vmem_limit_bytes=16 * MIB),
+        name="relay",
+    )(gate_up, down, combine)
+    partner = lax.ppermute(to_partner, "core", swap)
+
     got = lax.all_to_all(outgoing.reshape(z_size, 2 * x_size, lanes), "z", 0, 0, tiled=True)
-    (spread,) = run(spread_kernel, "spread", [((y_size, slots, lanes), bf16)])(
-        got.reshape(slots, lanes)
-    )
+    got, gate_up, halves = lax.optimization_barrier((got, gate_up, halves))
+    (spread,) = run(spread_kernel, [((y_size, slots, lanes), bf16)])(got.reshape(slots, lanes))
     mine = lax.all_to_all(
         spread.reshape(y_size * x_size, 2 * z_size, lanes), PLANE, 0, 0, tiled=True
     ).reshape(y_size, slots, lanes)
-    gate_up, down, mine = lax.optimization_barrier((gate_up, w_down[0], mine))
-    gate_up, sent_down = run(
-        relay_kernel,
-        "relay",
-        [((2, 2 * units, y_size * lanes), bf16), ((units, y_size * lanes), bf16)],
+
+    (projected,) = run(project_kernel, [((4 * units + 8, slots), jnp.float32)])(
+        mine, gate_up, partner
+    )
+    (kept_down,) = run(
+        keep_kernel,
+        [((units, width), bf16)],
         [pltpu.VMEM((units, features), bf16), pltpu.SemaphoreType.DMA],
-        from_hbm=(1,),
-    )(gate_up, pltpu.with_memory_space_constraint(down, pltpu.HBM))
-    theirs = lax.ppermute(mine, "core", swap)
-    act, sent = run(
-        expert_kernel,
-        "expert",
-        [((units, slots), bf16), ((y_size, slots, lanes), bf16)],
-        [pltpu.VMEM((2 * units, slots), jnp.float32)],
-    )(mine, theirs, gate_up, sent_down)
-
-    arrived = lax.ppermute(sent, "core", swap)
-    own, halves = run(
-        own_kernel,
-        "own",
-        [((y_size, slots, lanes), jnp.float32), ((2 * rows, slots), bf16)],
-    )(act, down, combine)
-    paired = (own + arrived.astype(jnp.float32)).astype(bf16)
+        from_hbm=(0,),
+    )(down, projected)
+    theirs = lax.ppermute(projected, "core", swap)
+    (paired,) = run(
+        down_kernel,
+        [((y_size, slots, lanes), bf16)],
+        [pltpu.VMEM((2, 2 * units, slots), jnp.float32)],
+    )(projected, theirs, kept_down, partner)
+
     paired = lax.all_to_all(
         paired.reshape(y_size * x_size, 2 * z_size, lanes), PLANE, 0, 0, tiled=True
     )
-    (summed,) = run(gather_kernel, "gather", [((slots, share), bf16)])(
-        paired.reshape(y_size, slots, lanes)
-    )
+    (summed,) = run(gather_kernel, [((slots, share), bf16)])(paired.reshape(y_size, slots, lanes))
     back = lax.all_to_all(summed.reshape(z_size, 2 * x_size, share), "z", 0, 0, tiled=True)
     return pl.pallas_call(
         finish_kernel,

time: 95.2 us -> 97.3 us (1.022)
  Pallas kernels: 7.41 us -> 9.07 us
  blocking collectives: 82.1 us -> 83.7 us
    pallas_call x0 -> x1, Pallas kernels: none -> 2.4 us  [local(): pl.pallas_call(relay_kernel, out_shape=(pltpu.VMEM((2 * units, width), bf...]
  transfers between devices with their start and end apart: 2 -> 2, of which waited for: 2 -> 1; matrix products, arithmetic and copies ran while one was open for 0% -> 0% of each run, Pallas kernels for 2% -> 2%
where the time goes in v5:
time: 97.3 us; the launch traced here: 96.9 us
  blocking collectives  83.7 us (86%)
  Pallas kernels  9.07 us (9%)
  starting transfers between devices  3.84 us (4%)
    all_to_all x1, blocking collectives, local(): lax.all_to_all(outgoing.reshape(z_size, 2 * x_size, lanes), 'z', 0, 0, ti...  28.6 us
    all_to_all x1, blocking collectives, local(): lax.all_to_all(summed.reshape(z_size, 2 * x_size, share), 'z', 0, 0, tile...  17 us
    all_to_all x1, blocking collectives, local(): lax.all_to_all(spread.reshape(y_size * x_size, 2 * z_size, lanes), PLANE,...  14.3 us
    all_to_all x1, blocking collectives, local(): lax.all_to_all(paired.reshape(y_size * x_size, 2 * z_size, lanes), PLANE,...  13.6 us
    all_to_all x1, blocking collectives, local(): parts = lax.all_to_all(parts, HEAD, 0, 0, tiled=True)  10.2 us
    pallas_call x6, Pallas kernels, call(): pl.pallas_call(kernel, out_shape=tuple((pltpu.VMEM(shape, dtype) for shap...  3.41 us
    pallas_call x1, Pallas kernels, attend(): pl.pallas_call(attend_kernel, out_shape=pltpu.VMEM((8, rows, features //...  2.51 us
    pallas_call x1, Pallas kernels, local(): pl.pallas_call(relay_kernel, out_shape=(pltpu.VMEM((2 * units, width), bf...  2.4 us
  transfers between devices with their start and end apart: 2, of which 1 were waited for; matrix products, arithmetic and copies ran while one was open for 0% of the time, Pallas kernels for 2%

profile of v5, /device:TPU:32, one launch (start us, length us, event | category | flops | bytes accessed | tf_op | source)
XLA Modules:
  0.0 96.9 jit_solution(16222353940791487609)
XLA Ops:
  0.0 0.0 copy-start.1
  0.0 2.5 %attend.1 = bf16[8,16,360]{2,1,0:T(8,128)(2,1)S(1)} custom-call(s32[1,16]{1,0:T(1,128)} %bitcast.39, f32[1,4]{1,0:T(1,128)} %sink_hbm.1, bf16[16,256]{1,0:T(8,128)(2,1)} %bitcast.37, bf16[16,128,128]{2,1,0:T(8,128)(2,1)} %bitcast.36, bf16[16,128]{1,0:T(8,128)(2,1)} %bitcast.38, bf16[2880,256]{1,0:T(8,128)(2,1)} %bitcast.35), custom_call_target="tpu_custom_call" | custom-call | tf_op jit(solution)/shard_map/attend/pallas_call | solution.py:130
  2.5 0.0 copy-start
  2.6 10.2 %all_to_all.25.parts_ref = bf16[8,16,360]{2,1,0:T(8,128)(2,1)S(1)} all-to-all(bf16[8,16,360]{2,1,0:T(8,128)(2,1)S(1)} %attend.1), channel_id=1, replica_groups=mesh['z'=16,'x'=4,'y'=4,'core'=2] {'y','core'}, dimensions={0} | all-to-all | bytes 184320 | tf_op jit(solution)/shard_map/all_to_all | solution.py:398
  12.8 0.0 copy-done.4
  12.8 0.0 copy-done.3
  12.8 0.0 copy-done.2
  12.8 0.0 copy-done.1
  12.8 0.4 shard_map.118
  13.2 2.4 %relay.1 = (bf16[360,1536]{1,0:T(8,128)(2,1)S(1)}, bf16[560,1536]{1,0:T(8,128)(2,1)}, bf16[32,128]{1,0:T(8,128)(2,1)S(1)}) custom-call(bf16[360,2880]{1,0:T(8,128)(2,1)S(1)} %bitcast.22, bf16[180,2880]{1,0:T(8,128)(2,1)} %bitcast.33, f32[128,16]{1,0:T(8,128)S(1)} %get-tuple-element.22.combine_ref), custom_call_target="tpu_custom_call" | custom-call | tf_op jit(solution)/shard_map/relay/pallas_call | solution.py:424
  15.6 1.9 %collective-permute-start = (bf16[560,1536]{1,0:T(8,128)(2,1)}, bf16[560,1536]{1,0:T(8,128)(2,1)S(1)}, u32[]{:S(2)}, u32[]{:S(2)}) collective-permute-start(bf16[560,1536]{1,0:T(8,128)(2,1)} %get-tuple-element.28), channel_id=1, source_target_pairs={{0,1},{1,0},{2,3},{3,2},{4,5},{5,4},{6,7},{7,6},{8,9},{9,8},{10,11... | collective-permute-start | bytes 5160968 | tf_op jit(solution)/shard_map/ppermute | solution.py:441
  17.5 28.6 %all_to_all.26 = bf16[16,8,384]{2,1,0:T(8,128)(2,1)S(1)} all-to-all(bf16[16,8,384]{2,1,0:T(8,128)(2,1)S(1)} %bitcast.30), channel_id=1, replica_groups=mesh['z'=16,'x'=4,'y'=4,'core'=2] {'z'}, dimensions={0} | all-to-all | bytes 196608 | tf_op jit(solution)/shard_map/all_to_all | solution.py:443
  46.1 0.2 shard_map.119
  46.3 14.3 %all_to_all.27 = bf16[16,32,384]{2,1,0:T(8,128)(2,1)S(1)} all-to-all(bf16[16,32,384]{2,1,0:T(8,128)(2,1)S(1)} %bitcast.23), channel_id=1, replica_groups=mesh['z'=16,'x'=4,'y'=4,'core'=2] {'y','x'}, dimensions={0} | all-to-all | bytes 786432 | tf_op jit(solution)/shard_map/all_to_all | solution.py:446
  60.5 0.0 collective-permute-done.partner_ref
  60.5 0.7 shard_map.120.after_ref.here_ref
  61.3 1.9 %collective-permute-start.1 = (f32[728,128]{1,0:T(8,128)S(1)}, f32[728,128]{1,0:T(8,128)S(1)}, u32[]{:S(2)}, u32[]{:S(2)}) collective-permute-start(f32[728,128]{1,0:T(8,128)S(1)} %shard_map.120.after_ref.here_ref), channel_id=1, source_target_pairs={{0,1},{1,0},{2,3},{3,2},{4,5},{5,4},{6,7},{7,6},{8,9},{9,8},{10,11... | collective-permute-start | bytes 1118216 | tf_op jit(solution)/shard_map/ppermute | solution.py:459
  63.2 1.5 %shard_map.121.down_ref = bf16[180,1536]{1,0:T(8,128)(2,1)S(1)} custom-call(bf16[180,2880]{1,0:T(8,128)(2,1)} %bitcast.34, f32[728,128]{1,0:T(8,128)S(1)} %shard_map.120.after_ref.here_ref), custom_call_target="tpu_custom_call" | custom-call | tf_op jit(solution)/shard_map/pallas_call | solution.py:362
  64.7 0.1 collective-permute-done.1.there_ref
  64.9 0.4 shard_map.122
  65.3 13.6 %all_to_all.28 = bf16[16,32,384]{2,1,0:T(8,128)(2,1)S(1)} all-to-all(bf16[16,32,384]{2,1,0:T(8,128)(2,1)S(1)} %bitcast.26), channel_id=1, replica_groups=mesh['z'=16,'x'=4,'y'=4,'core'=2] {'y','x'}, dimensions={0} | all-to-all | bytes 786432 | tf_op jit(solution)/shard_map/all_to_all | solution.py:466
  78.9 0.2 shard_map.123
  79.1 17.0 %all_to_all.29 = bf16[16,8,360]{2,1,0:T(8,128)(2,1)S(1)} all-to-all(bf16[16,8,360]{2,1,0:T(8,128)(2,1)S(1)} %bitcast.29), channel_id=1, replica_groups=mesh['z'=16,'x'=4,'y'=4,'core'=2] {'z'}, dimensions={0} | all-to-all | bytes 184320 | tf_op jit(solution)/shard_map/all_to_all | solution.py:470
  96.1 0.7 finish.1
  (4 shorter events, 0.0 us)
Async XLA Ops:
  0.0 12.8 %copy-start.4 = (s32[16,4]{0,1:T(4,128)S(1)}, s32[16,4]{0,1:T(4,128)}, u32[]{:S(2)}) copy-start(s32[16,4]{0,1:T(4,128)} %param.21) | copy-start | bytes 772
  0.0 12.8 %copy-start.3 = (s32[16,4]{0,1:T(4,128)S(1)}, s32[16,4]{0,1:T(4,128)}, u32[]{:S(2)}) copy-start(s32[16,4]{0,1:T(4,128)} %param.20) | copy-start | bytes 772
  0.0 12.8 %copy-start.2 = (f32[2880]{0:T(1024)S(1)}, f32[2880]{0:T(1024)}, u32[]{:S(2)}) copy-start(f32[2880]{0:T(1024)} %gain_ref.1) | copy-start | bytes 34564
  0.0 12.8 %copy-start.1 = (bf16[16,2880]{1,0:T(8,128)(2,1)S(1)}, bf16[16,2880]{1,0:T(8,128)(2,1)}, u32[]{:S(2)}) copy-start(bf16[16,2880]{1,0:T(8,128)(2,1)} %resid_ref.1) | copy-start | bytes 276484
  2.5 10.6 %copy-start = (bf16[1,2880,360]{1,2,0:T(8,128)(2,1)S(1)}, bf16[1,2880,360]{1,2,0:T(8,128)(2,1)}, u32[]{:S(2)}) copy-start(bf16[1,2880,360]{1,2,0:T(8,128)(2,1)} %param.22) | copy-start | bytes 6220804
  15.6 45.0 %collective-permute-start = (bf16[560,1536]{1,0:T(8,128)(2,1)}, bf16[560,1536]{1,0:T(8,128)(2,1)S(1)}, u32[]{:S(2)}, u32[]{:S(2)}) collective-permute-start(bf16[560,1536]{1,0:T(8,128)(2,1)} %get-tuple-element.28), channel_id=1, source_target_pairs={{0,1},{1,0},{2,3},{3,2},{4,5},{5,4},{6,7},{7,6},{8,9},{9,8},{10,11... | collective-permute-start | bytes 5160968 | tf_op jit(solution)/shard_map/ppermute | solution.py:441
  61.3 3.6 %collective-permute-start.1 = (f32[728,128]{1,0:T(8,128)S(1)}, f32[728,128]{1,0:T(8,128)S(1)}, u32[]{:S(2)}, u32[]{:S(2)}) collective-permute-start(f32[728,128]{1,0:T(8,128)S(1)} %shard_map.120.after_ref.here_ref), channel_id=1, source_target_pairs={{0,1},{1,0},{2,3},{3,2},{4,5},{5,4},{6,7},{7,6},{8,9},{9,8},{10,11... | collective-permute-start | bytes 1118216 | tf_op jit(solution)/shard_map/ppermute | solution.py:459

commit v6 on v5

--- a/solution.py
+++ b/solution.py
@@ -115,7 +115,7 @@
     merged = jnp.concatenate(merged, axis=1).astype(jnp.bfloat16)
     proj_copy.wait()
     for s in range(shares):
-        out_ref[s] = lax.dot_general(
+        out_ref[(s % 2) * (shares // 2) + s // 2] = lax.dot_general(
             merged,
             proj_ref[pl.ds(s * share_width, share_width), :],
             (((1,), (1,)), ((), ())),
@@ -291,10 +291,7 @@
     bottom.wait()
 
 
-def keep_kernel(down_hbm, after_ref, out_ref, down_ref, sem):
-    copy = pltpu.make_async_copy(down_hbm, down_ref, sem)
-    copy.start()
-    copy.wait()
+def keep_kernel(down_ref, after_ref, out_ref):
     for_core(lambda c: lay(down_ref[...], out_ref, 0, c))
 
 
@@ -302,18 +299,20 @@
     return jnp.concatenate([ref[y] for y in range(ref.shape[0])], axis=1)
 
 
-def project_kernel(mine_ref, up_ref, partner_ref, out_ref):
+def project_kernel(mine_ref, up_ref, partner_ref, later_hbm, out_ref, send_ref):
     y_size, slots, lanes = mine_ref.shape
     share = FEATURES // (2 * y_size)
     columns = up_ref.shape[0]
     x = joined(mine_ref)
     for block, ref in enumerate((up_ref, partner_ref)):
-        out_ref[pl.ds(block * columns, columns), :] = lax.dot_general(
+        found = lax.dot_general(
             ref[pl.ds(0, columns), :],
             x,
             (((1,), (1,)), ((), ())),
             preferred_element_type=jnp.float32,
         )
+        out_ref[pl.ds(block * columns, columns), :] = found
+        send_ref[pl.ds(block * columns, columns), :] = found.astype(jnp.bfloat16)
     squares = jnp.zeros((slots, 128), jnp.float32)
     for y in range(y_size):
         squares = squares + mine_ref[y, :, lanes - 128 :].astype(jnp.float32)
@@ -322,6 +321,12 @@
     squares = jnp.sum(jnp.transpose(squares), axis=0, keepdims=True)
     tail = out_ref.shape[0] - 2 * columns
     out_ref[pl.ds(2 * columns, tail), :] = jnp.broadcast_to(squares, (tail, slots))
+    tail = send_ref.shape[0] - 2 * columns
+    high = squares.astype(jnp.bfloat16).astype(jnp.float32)
+    first = lax.broadcasted_iota(jnp.int32, (tail, slots), 0) == 0
+    send_ref[pl.ds(2 * columns, tail), :] = jnp.where(first, high, squares - high).astype(
+        jnp.bfloat16
+    )
 
 
 def down_kernel(here_ref, there_ref, down_ref, partner_ref, out_ref, held_ref):
@@ -329,14 +334,13 @@
     columns = 2 * units
     y_size, _, lanes = out_ref.shape
     last = here_ref.shape[0] - 1
-    squares = here_ref[last : last + 1, :] + there_ref[last : last + 1, :]
+    tail = there_ref[pl.ds(2 * columns, there_ref.shape[0] - 2 * columns), :].astype(jnp.float32)
+    squares = here_ref[last : last + 1, :] + tail[0:1, :] + tail[1:2, :]
     scale = lax.rsqrt(squares / FEATURES + epsilon)
     total = jnp.zeros((out_ref.shape[1], y_size * lanes), jnp.float32)
     for block, weights in enumerate((down_ref[...], partner_ref[pl.ds(DOWN_AT, units), :])):
-        held_ref[block] = (
-            here_ref[pl.ds(block * columns, columns), :]
-            + there_ref[pl.ds((1 - block) * columns, columns), :]
-        ) * scale
+        theirs = there_ref[pl.ds((1 - block) * columns, columns), :].astype(jnp.float32)
+        held_ref[block] = (here_ref[pl.ds(block * columns, columns), :] + theirs) * scale
         gate = held_ref[block, pl.ds(0, units, stride=2), :]
         up = held_ref[block, pl.ds(1, units, stride=2), :]
         act = ((up + 1.0) * gate * jax.nn.sigmoid(swish_alpha * gate)).astype(jnp.bfloat16)
@@ -395,7 +399,7 @@
     swap = [(0, 1), (1, 0)]
 
     parts = attend(positions, sink_logits, queries, kv_cache, new_kv, out_proj)
-    parts = lax.all_to_all(parts, HEAD, 0, 0, tiled=True)
+    parts = lax.all_to_all(parts, ("core", "y"), 0, 0, tiled=True)
     gate_up = jnp.swapaxes(w_gate_up[0], 0, 1)
     hidden, outgoing, combine = run(
         dispatch_kernel,
@@ -447,16 +451,13 @@
         spread.reshape(y_size * x_size, 2 * z_size, lanes), PLANE, 0, 0, tiled=True
     ).reshape(y_size, slots, lanes)
 
-    (projected,) = run(project_kernel, [((4 * units + 8, slots), jnp.float32)])(
-        mine, gate_up, partner
-    )
-    (kept_down,) = run(
-        keep_kernel,
-        [((units, width), bf16)],
-        [pltpu.VMEM((units, features), bf16), pltpu.SemaphoreType.DMA],
-        from_hbm=(0,),
-    )(down, projected)
-    theirs = lax.ppermute(projected, "core", swap)
+    projected, to_swap = run(
+        project_kernel,
+        [((4 * units + 8, slots), jnp.float32), ((4 * units + 16, slots), bf16)],
+        from_hbm=(3,),
+    )(mine, gate_up, partner, pltpu.with_memory_space_constraint(w_down[0], pltpu.HBM))
+    (kept_down,) = run(keep_kernel, [((units, width), bf16)])(w_down[0], projected)
+    theirs = lax.ppermute(to_swap, "core", swap)
     (paired,) = run(
         down_kernel,
         [((y_size, slots, lanes), bf16)],

time: 97.3 us -> 96.7 us (level)
  Pallas kernels: 9.07 us -> 7.82 us
    pallas_call x6, Pallas kernels: 3.41 us -> 2.17 us  [call(): pl.pallas_call(kernel, out_shape=tuple((pltpu.VMEM(shape, dtype) for shap...]
  transfers between devices with their start and end apart: 2 -> 2, of which waited for: 1 -> 1; matrix products, arithmetic and copies ran while one was open for 0% -> 0% of each run, Pallas kernels for 2% -> 0%
where the time goes in v6:
time: 96.7 us; the launch traced here: 96.3 us
  blocking collectives  83.3 us (86%)
  Pallas kernels  7.82 us (8%)
  starting transfers between devices  3.96 us (4%)
  waiting for transfers between devices  1.11 us (1%)
    all_to_all x1, blocking collectives, local(): lax.all_to_all(outgoing.reshape(z_size, 2 * x_size, lanes), 'z', 0, 0, ti...  28.5 us
    all_to_all x1, blocking collectives, local(): lax.all_to_all(summed.reshape(z_size, 2 * x_size, share), 'z', 0, 0, tile...  17 us
    all_to_all x1, blocking collectives, local(): lax.all_to_all(spread.reshape(y_size * x_size, 2 * z_size, lanes), PLANE,...  14.7 us
    all_to_all x1, blocking collectives, local(): lax.all_to_all(paired.reshape(y_size * x_size, 2 * z_size, lanes), PLANE,...  13.3 us
    all_to_all x1, blocking collectives, local(): parts = lax.all_to_all(parts, ('core', 'y'), 0, 0, tiled=True)  9.8 us
    pallas_call x1, Pallas kernels, attend(): pl.pallas_call(attend_kernel, out_shape=pltpu.VMEM((8, rows, features //...  2.51 us
    pallas_call x1, Pallas kernels, local(): pl.pallas_call(relay_kernel, out_shape=(pltpu.VMEM((2 * units, width), bf...  2.39 us
    pallas_call x6, Pallas kernels, call(): pl.pallas_call(kernel, out_shape=tuple((pltpu.VMEM(shape, dtype) for shap...  2.17 us
  transfers between devices with their start and end apart: 2, of which 1 were waited for; matrix products, arithmetic and copies ran while one was open for 0% of the time, Pallas kernels for 0%

profile of v6, /device:TPU:32, one launch (start us, length us, event | category | flops | bytes accessed | tf_op | source)
XLA Modules:
  0.0 96.3 jit_solution(8341414197038578664)
XLA Ops:
  0.0 0.0 copy-start.2
  0.0 2.5 %attend.1 = bf16[8,16,360]{2,1,0:T(8,128)(2,1)S(1)} custom-call(s32[1,16]{1,0:T(1,128)} %bitcast.40, f32[1,4]{1,0:T(1,128)} %sink_hbm.1, bf16[16,256]{1,0:T(8,128)(2,1)} %bitcast.38, bf16[16,128,128]{2,1,0:T(8,128)(2,1)} %bitcast.37, bf16[16,128]{1,0:T(8,128)(2,1)} %bitcast.39, bf16[2880,256]{1,0:T(8,128)(2,1)} %bitcast.36), custom_call_target="tpu_custom_call" | custom-call | tf_op jit(solution)/shard_map/attend/pallas_call | solution.py:130
  2.5 0.0 copy-start.1
  2.6 9.8 %all_to_all.25.parts_ref = bf16[8,16,360]{2,1,0:T(8,128)(2,1)S(1)} all-to-all(bf16[8,16,360]{2,1,0:T(8,128)(2,1)S(1)} %attend.1), channel_id=1, replica_groups=mesh['z'=16,'x'=4,'y'=4,'core'=2] {'core','y'}, dimensions={0} | all-to-all | bytes 184320 | tf_op jit(solution)/shard_map/all_to_all | solution.py:402
  12.4 0.0 copy-done.5
  12.4 0.0 copy-done.4
  12.4 0.0 copy-done.3
  12.4 0.0 copy-done.2
  12.4 0.4 shard_map.118
  12.8 2.4 %relay.1 = (bf16[360,1536]{1,0:T(8,128)(2,1)S(1)}, bf16[560,1536]{1,0:T(8,128)(2,1)}, bf16[32,128]{1,0:T(8,128)(2,1)S(1)}) custom-call(bf16[360,2880]{1,0:T(8,128)(2,1)S(1)} %bitcast.25, bf16[180,2880]{1,0:T(8,128)(2,1)} %bitcast.21, f32[128,16]{1,0:T(8,128)S(1)} %get-tuple-element.24.combine_ref), custom_call_target="tpu_custom_call" | custom-call | tf_op jit(solution)/shard_map/relay/pallas_call | solution.py:428
  15.2 2.0 %collective-permute-start = (bf16[560,1536]{1,0:T(8,128)(2,1)}, bf16[560,1536]{1,0:T(8,128)(2,1)S(1)}, u32[]{:S(2)}, u32[]{:S(2)}) collective-permute-start(bf16[560,1536]{1,0:T(8,128)(2,1)} %get-tuple-element.30), channel_id=1, source_target_pairs={{0,1},{1,0},{2,3},{3,2},{4,5},{5,4},{6,7},{7,6},{8,9},{9,8},{10,11... | collective-permute-start | bytes 5160968 | tf_op jit(solution)/shard_map/ppermute | solution.py:445
  17.2 28.5 %all_to_all.26 = bf16[16,8,384]{2,1,0:T(8,128)(2,1)S(1)} all-to-all(bf16[16,8,384]{2,1,0:T(8,128)(2,1)S(1)} %bitcast.33), channel_id=1, replica_groups=mesh['z'=16,'x'=4,'y'=4,'core'=2] {'z'}, dimensions={0} | all-to-all | bytes 196608 | tf_op jit(solution)/shard_map/all_to_all | solution.py:447
  45.7 0.2 shard_map.119
  45.8 14.7 %all_to_all.27 = bf16[16,32,384]{2,1,0:T(8,128)(2,1)S(1)} all-to-all(bf16[16,32,384]{2,1,0:T(8,128)(2,1)S(1)} %bitcast.27), channel_id=1, replica_groups=mesh['z'=16,'x'=4,'y'=4,'core'=2] {'y','x'}, dimensions={0} | all-to-all | bytes 786432 | tf_op jit(solution)/shard_map/all_to_all | solution.py:450
  60.5 0.0 collective-permute-done.partner_ref
  60.5 0.7 shard_map.120
  61.3 1.9 %collective-permute-start.1 = (bf16[736,128]{1,0:T(8,128)(2,1)S(1)}, bf16[736,128]{1,0:T(8,128)(2,1)S(1)}, u32[]{:S(2)}, u32[]{:S(2)}) collective-permute-start(bf16[736,128]{1,0:T(8,128)(2,1)S(1)} %get-tuple-element.32), channel_id=1, source_target_pairs={{0,1},{1,0},{2,3},{3,2},{4,5},{5,4},{6,7},{7,6},{8,9},{9,8},{10,11... | collective-permute-start | bytes 565256 | tf_op jit(solution)/shard_map/ppermute | solution.py:460
  63.2 0.3 shard_map.121.down_ref
  63.5 1.1 %collective-permute-done.1.there_ref = bf16[736,128]{1,0:T(8,128)(2,1)S(1)} collective-permute-done((bf16[736,128]{1,0:T(8,128)(2,1)S(1)}, bf16[736,128]{1,0:T(8,128)(2,1)S(1)}, u32[]{:S(2)}, u32[]{:S(2)}) %collective-permute-start.1) | collective-permute-done | bytes 188448 | tf_op jit(solution)/shard_map/ppermute | solution.py:460
  64.6 0.4 shard_map.122
  65.0 13.3 %all_to_all.28 = bf16[16,32,384]{2,1,0:T(8,128)(2,1)S(1)} all-to-all(bf16[16,32,384]{2,1,0:T(8,128)(2,1)S(1)} %bitcast.26), channel_id=1, replica_groups=mesh['z'=16,'x'=4,'y'=4,'core'=2] {'y','x'}, dimensions={0} | all-to-all | bytes 786432 | tf_op jit(solution)/shard_map/all_to_all | solution.py:467
  78.3 0.2 shard_map.123
  78.5 17.0 %all_to_all.29 = bf16[16,8,360]{2,1,0:T(8,128)(2,1)S(1)} all-to-all(bf16[16,8,360]{2,1,0:T(8,128)(2,1)S(1)} %bitcast.32), channel_id=1, replica_groups=mesh['z'=16,'x'=4,'y'=4,'core'=2] {'z'}, dimensions={0} | all-to-all | bytes 184320 | tf_op jit(solution)/shard_map/all_to_all | solution.py:471
  95.6 0.7 finish.1
  (6 shorter events, 0.0 us)
Async XLA Ops:
  0.0 12.4 %copy-start.5 = (s32[16,4]{0,1:T(4,128)S(1)}, s32[16,4]{0,1:T(4,128)}, u32[]{:S(2)}) copy-start(s32[16,4]{0,1:T(4,128)} %param.21) | copy-start | bytes 772
  0.0 12.4 %copy-start.4 = (s32[16,4]{0,1:T(4,128)S(1)}, s32[16,4]{0,1:T(4,128)}, u32[]{:S(2)}) copy-start(s32[16,4]{0,1:T(4,128)} %param.20) | copy-start | bytes 772
  0.0 12.4 %copy-start.3 = (f32[2880]{0:T(1024)S(1)}, f32[2880]{0:T(1024)}, u32[]{:S(2)}) copy-start(f32[2880]{0:T(1024)} %gain_ref.1) | copy-start | bytes 34564
  0.0 12.4 %copy-start.2 = (bf16[16,2880]{1,0:T(8,128)(2,1)S(1)}, bf16[16,2880]{1,0:T(8,128)(2,1)}, u32[]{:S(2)}) copy-start(bf16[16,2880]{1,0:T(8,128)(2,1)} %resid_ref.1) | copy-start | bytes 276484
  2.5 10.2 %copy-start.1 = (bf16[1,2880,360]{1,2,0:T(8,128)(2,1)S(1)}, bf16[1,2880,360]{1,2,0:T(8,128)(2,1)}, u32[]{:S(2)}) copy-start(bf16[1,2880,360]{1,2,0:T(8,128)(2,1)} %param.22) | copy-start | bytes 6220804
  15.2 45.4 %collective-permute-start = (bf16[560,1536]{1,0:T(8,128)(2,1)}, bf16[560,1536]{1,0:T(8,128)(2,1)S(1)}, u32[]{:S(2)}, u32[]{:S(2)}) collective-permute-start(bf16[560,1536]{1,0:T(8,128)(2,1)} %get-tuple-element.30), channel_id=1, source_target_pairs={{0,1},{1,0},{2,3},{3,2},{4,5},{5,4},{6,7},{7,6},{8,9},{9,8},{10,11... | collective-permute-start | bytes 5160968 | tf_op jit(solution)/shard_map/ppermute | solution.py:445
  60.5 2.7 %copy-start = (bf16[1,180,2880]{2,1,0:T(8,128)(2,1)S(1)}, bf16[1,180,2880]{2,1,0:T(8,128)(2,1)}, u32[]{:S(2)}) copy-start(bf16[1,180,2880]{2,1,0:T(8,128)(2,1)} %param.23) | copy-start | bytes 3110404
  61.3 3.3 %collective-permute-start.1 = (bf16[736,128]{1,0:T(8,128)(2,1)S(1)}, bf16[736,128]{1,0:T(8,128)(2,1)S(1)}, u32[]{:S(2)}, u32[]{:S(2)}) collective-permute-start(bf16[736,128]{1,0:T(8,128)(2,1)S(1)} %get-tuple-element.32), channel_id=1, source_target_pairs={{0,1},{1,0},{2,3},{3,2},{4,5},{5,4},{6,7},{7,6},{8,9},{9,8},{10,11... | collective-permute-start | bytes 565256 | tf_op jit(solution)/shard_map/ppermute | solution.py:460
